TPU v7x, 32 devices: a 4x4x1 block of a 4x4x8 slice. The times are simulated.
32 devices in a mesh: dp: 1 (over z), tp: 32 (over y, x, core).
Axes of the slice: x: 4, y: 4, z: 1, core: 2. Of those that a mesh axis runs over, the one named last changes fastest.
The devices are a block of a 4x4x8 slice.
Arguments:
- x_norm: bfloat16 [2048, 4096], P(('dp', 'tp'))
- grad_y: bfloat16 [2048, 4096], P(('dp', 'tp'))
- u_gate: bfloat16 [2048, 11008], P('dp', 'tp')
- u_up: bfloat16 [2048, 11008], P('dp', 'tp')
- w_gate: bfloat16 [4096, 11008], P(None, 'tp')
- w_up: bfloat16 [4096, 11008], P(None, 'tp')
- w_down: bfloat16 [11008, 4096], P('tp')
- x_in: bfloat16 [2048, 4096], P(('dp', 'tp'))
- gamma: bfloat16 [4096], replicated
- grad_res: bfloat16 [2048, 4096], P(('dp', 'tp'))
- attn_out: bfloat16 [2048, 4096], P('dp', 'tp')
- w_out: bfloat16 [4096, 4096], P('tp')
Outputs:
- output 1: bfloat16 [2048, 4096], P(('dp', 'tp'))
- output 2: bfloat16 [2048, 4096], P('dp', 'tp')
- output 3: float32 [4096, 11008], P('dp', 'tp')
- output 4: float32 [4096, 11008], P('dp', 'tp')
- output 5: float32 [11008, 4096], P(('dp', 'tp'))
- output 6: float32 [4096, 4096], P(('dp', 'tp'))
All inputs are finite; a program needn't handle non-finite values.
Results may differ from a plain program's by a relative error of at most 0.0158273.
Values are sent between devices in bfloat16 or wider.
A program may use at most 768 MiB of HBM per device.

v0:
```python
import jax
import jax.numpy as jnp
from jax import lax
from jax.sharding import PartitionSpec as P

NORM_EPS = 1e-5
CONTRACT_ROWS = (((0,), (0,)), ((), ()))
CONTRACT_COLS = (((1,), (1,)), ((), ()))


def rms_backward(grad_x, x_in, gamma, grad_res):
    xin_f = x_in.astype(jnp.float32)
    inv_rms = lax.rsqrt(jnp.mean(xin_f * xin_f, axis=-1, keepdims=True) + NORM_EPS)
    scaled = grad_x.astype(jnp.float32) * gamma.astype(jnp.float32)
    proj_mean = jnp.mean(scaled * xin_f, axis=-1, keepdims=True)
    return (grad_res.astype(jnp.float32)
            + inv_rms * (scaled - xin_f * (inv_rms * inv_rms) * proj_mean)).astype(jnp.bfloat16)


def solution(mesh):
    token_spec = P(("dp", "tp"), None)
    split_cols = P("dp", "tp")
    weight_cols = P(None, "tp")
    weight_rows = P("tp", None)

    def local_backward(x_norm, grad_y, u_gate, u_up, w_gate, w_up, w_down, x_in, gamma, grad_res, attn_out, w_out):
        x_full = lax.all_gather(x_norm, "tp", axis=0, tiled=True)
        gy_full = lax.all_gather(grad_y, "tp", axis=0, tiled=True)
        gate_f = u_gate.astype(jnp.float32)
        up_f = u_up.astype(jnp.float32)
        sig_gate = jax.nn.sigmoid(gate_f)
        act_gate = gate_f * sig_gate
        silu_grad = sig_gate * (1.0 + gate_f * (1.0 - sig_gate))
        hidden_z = (act_gate * up_f).astype(jnp.bfloat16)
        gw_down = lax.dot_general(hidden_z, gy_full, CONTRACT_ROWS, preferred_element_type=jnp.float32)
        grad_h = lax.dot_general(gy_full, w_down, CONTRACT_COLS, preferred_element_type=jnp.float32)
        grad_up = (grad_h * act_gate).astype(jnp.bfloat16)
        grad_gate = (grad_h * up_f * silu_grad).astype(jnp.bfloat16)
        part_x = (lax.dot_general(grad_gate, w_gate, CONTRACT_COLS, preferred_element_type=jnp.float32)
                  + lax.dot_general(grad_up, w_up, CONTRACT_COLS, preferred_element_type=jnp.float32))
        grad_x = lax.psum_scatter(part_x.astype(jnp.bfloat16), "tp", scatter_dimension=0, tiled=True)
        gw_gate = lax.dot_general(x_full, grad_gate, CONTRACT_ROWS, preferred_element_type=jnp.float32)
        gw_up = lax.dot_general(x_full, grad_up, CONTRACT_ROWS, preferred_element_type=jnp.float32)
        grad_sum = rms_backward(grad_x, x_in, gamma, grad_res)
        gs_full = lax.all_gather(grad_sum, "tp", axis=0, tiled=True)
        grad_attn = lax.dot_general(gs_full, w_out, CONTRACT_COLS, preferred_element_type=jnp.float32).astype(jnp.bfloat16)
        gw_out = lax.dot_general(attn_out, gs_full, CONTRACT_ROWS, preferred_element_type=jnp.float32)
        return grad_sum, grad_attn, gw_gate, gw_up, gw_down, gw_out

    return jax.shard_map(
        local_backward,
        mesh=mesh,
        in_specs=(token_spec, token_spec, split_cols, split_cols, weight_cols, weight_cols, weight_rows,
                  token_spec, P(None), token_spec, split_cols, weight_rows),
        out_specs=(token_spec, split_cols, split_cols, split_cols, token_spec, token_spec),
        check_vma=False,
    )
```

profile of v0, /device:TPU:97, one launch (start us, length us, event | category | flops | bytes accessed | tf_op | source)
XLA Modules:
  0.0 406.5 jit_solution(3587899818291866608)
XLA Ops:
  7.2 0.0 copy-start
  7.2 0.1 all-gather.4.cloned.1.call-start
  7.3 0.7 all-gather.4.cloned.1.call-update
  8.0 0.1 reduce-scatter.2.cloned.1.call-start
  8.1 73.6 %all-gather.4.cloned.1.call-done = bf16[2048,4096]{1,0:T(8,128)(2,1)} async-done(((bf16[64,4096]{1,0:T(8,128)(2,1)}), bf16[2048,4096]{1,0:T(8,128)(2,1)}) %all-gather.4.cloned.1.call-update) | async-done | bytes 16777232 | tf_op jit(solution)/shard_map/all_gather | solution.py:28
  81.7 12.7 %fusion.1 = (bf16[2048,344]{0,1:T(8,128)(2,1)S(1)}, f32[2048,344]{0,1:T(8,128)}) fusion(bf16[2048,344]{0,1:T(8,128)(2,1)} %param.15, bf16[2048,344]{0,1:T(8,128)(2,1)} %param.14, bf16[2048,4096]{1,0:T(8,128)(2,1)} %all-gather.4.cloned.1.call-done, bf16[344,4096]{1,0:T(8,128)(2,1)} %param.18), kind=kOutput, calls=%fused_computation.10 | convolution fusion | flops 5779816448 | bytes 26640384 | tf_op jit(solution)/shard_map/dot_general | solution.py:36
  94.4 15.4 %fusion.19 = f32[2048,4096]{1,0:T(8,128)} fusion(bf16[2048,344]{0,1:T(8,128)(2,1)S(1)} %get-tuple-element.16, bf16[4096,344]{0,1:T(8,128)(2,1)S(1)} %copy-done), kind=kOutput, calls=%fused_computation.35 | convolution fusion | flops 5771362304 | bytes 37781504 | tf_op jit(solution)/shard_map/dot_general | solution.py:39
  109.8 23.6 %add_convert_fusion = bf16[2048,4096]{1,0:T(8,128)(2,1)} fusion(f32[2048,4096]{1,0:T(8,128)} %fusion.19, bf16[4096,344]{0,1:T(8,128)(2,1)} %param.17, f32[2048,344]{0,1:T(8,128)} %get-tuple-element.17, bf16[2048,344]{0,1:T(8,128)(2,1)} %param.14), kind=kOutput, calls=%fused_computation | convolution fusion | flops 5793071104 | bytes 57376768 | tf_op jit(solution)/shard_map/dot_general | solution.py:40
  133.4 0.1 reduce-scatter.2.cloned.1.call-update
  133.4 0.1 all-gather.8.cloned.1.call-start
  133.5 0.7 all-gather.8.cloned.1.call-update
  134.2 0.2 all-gather.6.cloned.1.call-start
  134.5 104.0 %reduce-scatter.2.cloned.1.call-done = bf16[64,4096]{1,0:T(8,128)(2,1)} async-done(((bf16[2048,4096]{1,0:T(8,128)(2,1)}), bf16[64,4096]{1,0:T(8,128)(2,1)}) %reduce-scatter.2.cloned.1.call-update) | async-done | bytes 524304 | tf_op jit(solution)/shard_map/reduce_scatter | solution.py:41
  238.5 1.4 fusion.10
  239.9 2.2 fusion.15
  242.1 0.1 all-gather.6.cloned.1.call-update
  242.2 67.1 %all-gather.8.cloned.1.call-done = bf16[2048,4096]{1,0:T(8,128)(2,1)} async-done(((bf16[64,4096]{1,0:T(8,128)(2,1)}), bf16[2048,4096]{1,0:T(8,128)(2,1)}) %all-gather.8.cloned.1.call-update) | async-done | bytes 16777232 | tf_op jit(solution)/shard_map/all_gather | solution.py:27
  309.3 12.2 %convolution_bitcast_fusion.1 = f32[4096,344]{0,1:T(8,128)} fusion(bf16[2048,344]{0,1:T(8,128)(2,1)S(1)} %copy-done.4, bf16[2048,4096]{1,0:T(8,128)(2,1)} %all-gather.8.cloned.1.call-done), kind=kOutput, calls=%fused_computation.2 | convolution fusion | flops 5771362304 | bytes 23822336 | tf_op jit(solution)/shard_map/dot_general | solution.py:42
  321.5 12.4 %fusion.8 = f32[344,4096]{1,0:T(8,128)} fusion(bf16[2048,4096]{1,0:T(8,128)(2,1)} %all-gather.4.cloned.1.call-done, bf16[2048,344]{0,1:T(8,128)(2,1)S(1)} %copy-done.9, bf16[2048,344]{0,1:T(8,128)(2,1)S(1)} %copy-done.6), kind=kOutput, calls=%fused_computation.22 | convolution fusion | flops 5776998400 | bytes 25231360 | tf_op jit(solution)/shard_map/dot_general | solution.py:35
  334.0 8.0 %convolution_bitcast_fusion = f32[4096,344]{0,1:T(8,128)} fusion(bf16[2048,4096]{1,0:T(8,128)(2,1)S(1)} %bitcast.20, f32[2048,344]{0,1:T(8,128)S(1)} %copy-done.2, bf16[2048,344]{0,1:T(8,128)(2,1)S(1)} %copy-done.6), kind=kOutput, calls=%fused_computation.1 | convolution fusion | flops 5776293888 | bytes 26640384 | tf_op jit(solution)/shard_map/dot_general | solution.py:43
  341.9 36.5 %all-gather.6.cloned.1.call-done = bf16[2048,4096]{1,0:T(8,128)(2,1)} async-done(((bf16[64,4096]{1,0:T(8,128)(2,1)}), bf16[2048,4096]{1,0:T(8,128)(2,1)}) %all-gather.6.cloned.1.call-update) | async-done | bytes 16777232 | tf_op jit(solution)/shard_map/all_gather | solution.py:45
  378.5 8.2 %convolution_bitcast_fusion.2 = f32[128,4096]{0,1:T(8,128)S(1)} fusion(bf16[2048,4096]{1,0:T(8,128)(2,1)} %all-gather.6.cloned.1.call-done, bf16[2048,128]{1,0:T(8,128)(2,1)S(1)} %copy-done.10), kind=kOutput, calls=%fused_computation.3 | convolution fusion | flops 2147483648 | bytes 19398656 | tf_op jit(solution)/shard_map/dot_general | solution.py:47
  386.7 1.8 copy.18
  388.5 11.5 %convolution_convert_fusion = bf16[2048,128]{1,0:T(8,128)(2,1)} fusion(bf16[2048,4096]{1,0:T(8,128)(2,1)} %all-gather.6.cloned.1.call-done, bf16[128,4096]{1,0:T(8,128)(2,1)} %param.23), kind=kOutput, calls=%fused_computation.18 | convolution fusion | flops 2147745792 | bytes 18350080 | tf_op jit(solution)/shard_map/dot_general | solution.py:46
  (33 shorter events, 0.1 us)
Async XLA Ops:
  7.2 87.2 %copy-start = (bf16[4096,344]{0,1:T(8,128)(2,1)S(1)}, bf16[4096,344]{0,1:T(8,128)(2,1)}, u32[]{:S(2)}) copy-start(bf16[4096,344]{0,1:T(8,128)(2,1)} %param.16) | copy-start | bytes 8454148
  7.2 74.5 %all-gather.4.cloned.1.call-start = ((), (), s32[]{:S(2)}) async-start(), calls=%async_computation.1 | async-start | bytes 17301504 | tf_op jit(solution)/shard_map/all_gather | solution.py:28
  8.0 230.5 %reduce-scatter.2.cloned.1.call-start = ((), (), s32[]{:S(2)}) async-start(), calls=%async_computation.2 | async-start | bytes 17301504 | tf_op jit(solution)/shard_map/reduce_scatter | solution.py:41
  94.4 15.4 %copy-start.3 = (bf16[2048,344]{0,1:T(8,128)(2,1)}, bf16[2048,344]{0,1:T(8,128)(2,1)S(1)}, u32[]{:S(2)}) copy-start(bf16[2048,344]{0,1:T(8,128)(2,1)S(1)} %get-tuple-element.16) | copy-start | bytes 4227076
  133.4 1.1 copy-start.8
  133.4 105.1 %copy-start.5 = (bf16[64,4096]{1,0:T(8,128)(2,1)S(1)}, bf16[64,4096]{1,0:T(8,128)(2,1)}, u32[]{:S(2)}) copy-start(bf16[64,4096]{1,0:T(8,128)(2,1)} %param.19) | copy-start | bytes 1572868
  133.4 106.5 %copy-start.7 = (bf16[64,4096]{1,0:T(8,128)(2,1)S(1)}, bf16[64,4096]{1,0:T(8,128)(2,1)}, u32[]{:S(2)}) copy-start(bf16[64,4096]{1,0:T(8,128)(2,1)} %param.21) | copy-start | bytes 1572868
  133.4 175.8 %copy-start.4 = (bf16[2048,344]{0,1:T(8,128)(2,1)S(1)}, bf16[2048,344]{0,1:T(8,128)(2,1)}, u32[]{:S(2)}) copy-start(bf16[2048,344]{0,1:T(8,128)(2,1)} %copy-done.3) | copy-start | bytes 4227076
  133.4 175.8 %all-gather.8.cloned.1.call-start = ((), (), s32[]{:S(2)}) async-start(), calls=%async_computation.4 | async-start | bytes 17301504 | tf_op jit(solution)/shard_map/all_gather | solution.py:27
  134.2 244.2 %all-gather.6.cloned.1.call-start = ((), (), s32[]{:S(2)}) async-start(), calls=%async_computation.3 | async-start | bytes 17301504 | tf_op jit(solution)/shard_map/all_gather | solution.py:45
  309.3 12.2 %copy-start.6 = (bf16[2048,344]{0,1:T(8,128)(2,1)S(1)}, bf16[2048,344]{0,1:T(8,128)(2,1)}, u32[]{:S(2)}) copy-start(bf16[2048,344]{0,1:T(8,128)(2,1)} %param.14) | copy-start | bytes 4227076
  309.3 12.2 %copy-start.9 = (bf16[2048,344]{0,1:T(8,128)(2,1)S(1)}, bf16[2048,344]{0,1:T(8,128)(2,1)}, u32[]{:S(2)}) copy-start(bf16[2048,344]{0,1:T(8,128)(2,1)} %param.15) | copy-start | bytes 4227076
  309.3 24.7 %slice-start = ((s8[16777216]{0:T(1024)(128)(4,1)}), s8[4194304]{0:T(1024)(128)(4,1)S(1)}, s32[]{:S(2)}) async-start(s8[16777216]{0:T(1024)(128)(4,1)} %bitcast.19), calls=%async_computation.5 | async-start | bytes 8388608
  309.3 24.7 %slice-start.1 = ((s8[16777216]{0:T(1024)(128)(4,1)}), s8[4194304]{0:T(1024)(128)(4,1)S(1)}, s32[]{:S(2)}) async-start(s8[16777216]{0:T(1024)(128)(4,1)} %bitcast.19), calls=%async_computation.6 | async-start | bytes 8388608
  309.3 24.7 %slice-start.2 = ((s8[16777216]{0:T(1024)(128)(4,1)}), s8[4194304]{0:T(1024)(128)(4,1)S(1)}, s32[]{:S(2)}) async-start(s8[16777216]{0:T(1024)(128)(4,1)} %bitcast.19), calls=%async_computation.7 | async-start | bytes 8388608
  321.5 12.4 %copy-start.2 = (f32[2048,344]{0,1:T(8,128)S(1)}, f32[2048,344]{0,1:T(8,128)}, u32[]{:S(2)}) copy-start(f32[2048,344]{0,1:T(8,128)} %get-tuple-element.17) | copy-start | bytes 8454148
  321.5 12.4 %slice-start.3 = ((s8[16777216]{0:T(1024)(128)(4,1)}), s8[4194304]{0:T(1024)(128)(4,1)S(1)}, s32[]{:S(2)}) async-start(s8[16777216]{0:T(1024)(128)(4,1)} %bitcast.19), calls=%async_computation.8 | async-start | bytes 8388608
  334.0 44.5 %copy-start.10 = (bf16[2048,128]{1,0:T(8,128)(2,1)S(1)}, bf16[2048,128]{1,0:T(8,128)(2,1)}, u32[]{:S(2)}) copy-start(bf16[2048,128]{1,0:T(8,128)(2,1)} %param.22) | copy-start | bytes 1572868
  388.5 11.5 %copy-start.1 = (bf16[4096,344]{0,1:T(8,128)(2,1)S(1)}, bf16[4096,344]{0,1:T(8,128)(2,1)}, u32[]{:S(2)}) copy-start(bf16[4096,344]{0,1:T(8,128)(2,1)} %param.16) | copy-start | bytes 8454148
Sparse Core Ops, SparseCore 0:
  10.1 71.5 all-gather.3
  133.5 104.8 reduce-scatter.1
  240.6 68.6 all-gather.7
  311.8 66.6 all-gather.5
where the time goes:
time: 407 us
  waiting for transfers between devices  283 us (70%)
  matrix products  104 us (26%)
  between operations  13.9 us (3%)
    reduce_scatter x1, waiting for transfers between devices, local_backward(): lax.psum_scatter(part_x.astype(jnp.bfloat16), 'tp', scatter_dimension=0,...  104 us
    all_gather x1, waiting for transfers between devices, local_backward(): gy_full = lax.all_gather(grad_y, 'tp', axis=0, tiled=True)  73.6 us
    all_gather x1, waiting for transfers between devices, local_backward(): x_full = lax.all_gather(x_norm, 'tp', axis=0, tiled=True)  67.1 us
    all_gather x1, waiting for transfers between devices, local_backward(): gs_full = lax.all_gather(grad_sum, 'tp', axis=0, tiled=True)  36.5 us
    dot_general x1, matrix products, local_backward(): lax.dot_general(grad_up, w_up, CONTRACT_COLS, preferred_element_type=jnp....  23.6 us
    dot_general x1, matrix products, local_backward(): lax.dot_general(grad_gate, w_gate, CONTRACT_COLS, preferred_element_type=...  15.4 us
    dot_general x1, matrix products, local_backward(): lax.dot_general(gy_full, w_down, CONTRACT_COLS, preferred_element_type=jn...  12.7 us
    dot_general x1, matrix products, local_backward(): lax.dot_general(hidden_z, gy_full, CONTRACT_ROWS, preferred_element_type=...  12.4 us
  transfers between devices with their start and end apart: 4, of which 4 were waited for; matrix products, arithmetic and copies ran while one was open for 9% of the time, Pallas kernels for 0%

commit v1 on v0

v1 whole, which is shorter than its diff:
```python
import functools
import math

import jax
import jax.numpy as jnp
from jax import lax
from jax.experimental import pallas as pl
from jax.experimental.pallas import tpu as pltpu
from jax.sharding import PartitionSpec as P

NORM_EPS = 1e-5
F32, BF16 = jnp.float32, jnp.bfloat16
LAG_X = 3
LAG_R = 2
SUBS = 4
SLOTS = 6
NN = (((1,), (0,)), ((), ()))
NT = (((1,), (1,)), ((), ()))
TN = (((0,), (0,)), ((), ()))


def dot(a, b, dims):
    return lax.dot_general(a, b, dims, preferred_element_type=F32)


def kernel(side, x_in_hbm, gy_in_hbm, ug_hbm, uu_hbm, wg_hbm, wu_hbm, wd_hbm, xin_hbm, gamma_hbm, gr_hbm, o_hbm, wo_hbm,
           ds_out, do_out, dwg_out, dwu_out, dwd_out, dwo_out,
           yb, xb, ugt, uut, ug, uu, wg, wu, wd, xin, gamma, gr, ov, wo,
           acc_g, acc_u, acc_d, acc_o, g_s, du_g, du_u, z_s, own_part, pp_send, pp_recv, rs_send, rs_recv, acc0,
           do_v, do_acc, o_pair,
           y_rs, y_rr, y_ps, y_pr, x_rs, x_rr, x_ps, x_pr,
           s_rs, s_rr, s_ps, s_pr, r_s, r_r, q_s, q_r, loc):
    n = side * side
    tok, hid = x_in_hbm.shape
    half = tok // 2
    ct = hid // 8
    sub_w = hid // SUBS

    me = lax.axis_index("tp")
    core = me % 2
    chip = me // 2
    cy, cx = chip // side, chip % side
    diag = (cx + cy) % side
    pos_own = side * (cy * (1 - core) + cx * core) + diag
    pos_par = side * (cx * (1 - core) + cy * core) + diag

    def index_of(e, q):
        a, b = q // side, q % side
        o = (b - a + side) % side
        yy = a * (1 - e) + o * e
        xx = o * (1 - e) + a * e
        return (yy * side + xx) * 2 + e

    partner = me + 1 - 2 * core
    nxt = (index_of(core, (pos_own + 1) % n), index_of(core, (pos_own + n - 1) % n))

    def token_row(s, rel, d):
        e = core if rel == 0 else 1 - core
        base = pos_own if rel == 0 else pos_par
        q = (base + n - s) % n if d == 0 else (base + s) % n
        return pl.multiple_of(index_of(e, q) * tok + half * d, half)

    def remote(src, dst, ssem, rsem, dev):
        return pltpu.make_async_remote_copy(src_ref=src, dst_ref=dst, send_sem=ssem, recv_sem=rsem,
                                            device_id={"tp": dev}, device_id_type=pl.DeviceIdType.MESH)

    def local(i):
        pairs = ((gy_in_hbm, yb.at[0, pl.ds(0, tok), :]), (x_in_hbm, xb.at[0, pl.ds(0, tok), :]),
                 (wd_hbm, wd), (ug_hbm, ugt), (uu_hbm, uut), (wg_hbm, wg), (wu_hbm, wu),
                 (xin_hbm, xin), (gamma_hbm, gamma), (gr_hbm, gr), (o_hbm, ov), (wo_hbm, wo),
                 (acc_d, dwd_out), (acc_g, dwg_out), (acc_u, dwu_out),
                 (yb.at[0, pl.ds(0, tok), :], ds_out), (do_v, do_out), (acc_o, dwo_out))
        return pltpu.make_async_copy(pairs[i][0], pairs[i][1], loc.at[i])

    for i in range(12):
        local(i).start()

    barrier = pltpu.get_barrier_semaphore()
    for dev in (nxt[0], nxt[1], partner):
        pl.semaphore_signal(barrier, inc=1, device_id={"tp": dev}, device_id_type=pl.DeviceIdType.MESH)
    pl.semaphore_wait(barrier, 3)

    def rows_at(s, rel, d):
        return pl.ds(pl.multiple_of((s % 2) * (2 * tok) + rel * tok + d * half, half), half)

    def ring_copy(b, ss, rr, s, d, cols=None):
        c = pl.ds(0, hid) if cols is None else cols
        return remote(b.at[(s // 2) % 3, rows_at(s, 0, d), c], b.at[((s + 1) // 2) % 3, rows_at(s + 1, 0, d), c],
                      ss(s, d), rr(s + 1, d), nxt[d])

    def pair_copy(b, ss, rr, s, d, cols=None):
        c = pl.ds(0, hid) if cols is None else cols
        return remote(b.at[(s // 2) % 3, rows_at(s, 0, d), c], b.at[(s // 2) % 3, rows_at(s, 1, d), c],
                      ss(s, d), rr(s, d), partner)

    def sem_of(arr):
        return lambda s, d: arr.at[d, s % SLOTS]

    def gather_service(b, sems, s, first):
        rs, rr, ps, pr = (sem_of(a) for a in sems)

        @pl.when(jnp.logical_and(s >= 2, s <= n + 1))
        def _():
            for d in range(2):
                pair_copy(b, ps, pr, s - 2, d).wait_send()

        @pl.when(jnp.logical_and(s >= 2, s <= n))
        def _():
            for d in range(2):
                ring_copy(b, rs, rr, s - 2, d).wait_send()

        @pl.when(s == 0)
        def _():
            local(first).wait()

        for d in range(2):
            @pl.when(jnp.logical_and(s >= 1, s <= n - 1))
            def _():
                ring_copy(b, rs, rr, s - 1, d).wait_recv()

            @pl.when(jnp.logical_and(s >= 0, s <= n - 2))
            def _():
                ring_copy(b, rs, rr, s, d).start()

            @pl.when(jnp.logical_and(s >= 0, s <= n - 1))
            def _():
                pair_copy(b, ps, pr, s, d).start()

        @pl.when(jnp.logical_and(s >= 0, s <= n - 1))
        def _():
            for d in range(2):
                pair_copy(b, ps, pr, s, d).wait_recv()

    y_sems, x_sems = (y_rs, y_rr, y_ps, y_pr), (x_rs, x_rr, x_ps, x_pr)

    def part_a(t):
        gather_service(yb, y_sems, t, 0)

    def part_b(t):
        gather_service(xb, x_sems, t - LAG_X, 1)

    def task_1(k):
        @pl.when(k == 0)
        def _():
            for i in (2, 3, 4):
                local(i).wait()

            def turn(c, carry):
                cols = pl.ds(pl.multiple_of(c * 128, 128), 128)
                ug[cols, :] = ugt[:, cols].astype(F32).T.astype(BF16)
                uu[cols, :] = uut[:, cols].astype(F32).T.astype(BF16)
                return carry
            lax.fori_loop(0, ug.shape[0] // 128, turn, 0)
        g_s[...] = dot(yb[k % 3], wd[...], NT)
        for i in range(2):
            for rel in range(2):
                for d in range(2):
                    r0 = i * 2 * tok + rel * tok + d * half
                    row = token_row(2 * k + i, rel, d)
                    gate = ug[pl.ds(row, half), :].astype(F32)
                    up = uu[pl.ds(row, half), :].astype(F32)
                    sig = jax.nn.sigmoid(gate)
                    act = gate * sig
                    grad = g_s[pl.ds(r0, half), :]
                    z_s[pl.ds(r0, half), :] = (act * up).astype(BF16)
                    du_u[k % 2, pl.ds(r0, half), :] = (grad * act).astype(BF16)
                    du_g[k % 2, pl.ds(r0, half), :] = (grad * up * (sig * (1.0 + gate * (1.0 - sig)))).astype(BF16)

    def pp_copy(k):
        return remote(pp_send.at[k % 2], pp_recv.at[k % 2], q_s.at[k % 2], q_r.at[k % 2], partner)

    def task_2(k, lo, hi):
        ks = k % 2
        if lo == 0:
            @pl.when(k == 0)
            def _():
                local(5).wait()
                local(6).wait()

            @pl.when(k >= 2)
            def _():
                pp_copy(k - 2).wait_send()

        def body(c, carry):
            cols = pl.ds(pl.multiple_of(c * ct, ct), ct)
            r = (dot(du_g[ks], wg[:, cols], NN) + dot(du_u[ks], wu[:, cols], NN)).astype(BF16)
            for i in range(2):
                own_part[ks, pl.ds(i * tok, tok), cols] = r[i * 2 * tok:i * 2 * tok + tok]
                pp_send[ks, pl.ds(i * tok, tok), cols] = r[i * 2 * tok + tok:(i + 1) * 2 * tok]
            return carry
        lax.fori_loop(lo, hi, body, 0)
        if hi == 8:
            pp_copy(k).start()

    def task_3(k):
        def body(c, carry):
            cols = pl.ds(pl.multiple_of(c * ct, ct), ct)
            acc_d[:, cols] += dot(z_s[...], yb[k % 3, :, cols], TN)
            return carry
        lax.fori_loop(0, 8, body, 0)

    def task_4(k):
        def body(c, carry):
            cols = pl.ds(pl.multiple_of(c * ct, ct), ct)
            xt = xb[k % 3, :, cols]
            acc_g[:, cols] += dot(du_g[k % 2], xt, TN)
            acc_u[:, cols] += dot(du_u[k % 2], xt, TN)
            return carry
        lax.fori_loop(0, 8, body, 0)

    def rs_copy(j, d):
        return remote(rs_send.at[j % 2, pl.ds(d * half, half), :], rs_recv.at[(j + 1) % 3, pl.ds(d * half, half), :],
                      r_s.at[d, j % 2], r_r.at[d, (j + 1) % 3], nxt[d])

    def part_d(t, i):
        j = t - LAG_R
        ks = (j // 2) % 2
        rows = pl.ds(i * tok, tok)
        if i == 0:
            @pl.when(jnp.logical_and(j >= 0, j <= n - 2))
            def _():
                pp_copy(j // 2).wait_recv()

            @pl.when(j == 0)
            def _():
                acc0[...] = own_part[ks, rows, :].astype(F32) + pp_recv[ks, rows, :].astype(F32)

        @pl.when(jnp.logical_and(j >= 3, j <= n + 1))
        def _():
            for d in range(2):
                rs_copy(j - 2, d).wait_send()

        for d in range(2):
            dr = pl.ds(d * half, half)
            pr = pl.ds(i * tok + d * half, half)

            @pl.when(jnp.logical_and(j >= 2, j <= n))
            def _():
                rs_copy(j - 1, d).wait_recv()

            @pl.when(j == 1)
            def _():
                rs_send[j % 2, dr, :] = (own_part[ks, pr, :].astype(F32) + pp_recv[ks, pr, :].astype(F32)).astype(BF16)

            @pl.when(jnp.logical_and(j >= 2, j <= n - 1))
            def _():
                rs_send[j % 2, dr, :] = (own_part[ks, pr, :].astype(F32) + pp_recv[ks, pr, :].astype(F32)
                                         + rs_recv[j % 3, dr, :].astype(F32)).astype(BF16)

            @pl.when(jnp.logical_and(j >= 1, j <= n - 1))
            def _():
                rs_copy(j, d).start()

    acc_d[...] = jnp.zeros_like(acc_d)
    acc_g[...] = jnp.zeros_like(acc_g)
    acc_u[...] = jnp.zeros_like(acc_u)
    acc_o[...] = jnp.zeros_like(acc_o)

    def pair_body(kk, carry):
        t = 2 * kk
        part_a(t)

        @pl.when(jnp.logical_and(kk >= 1, kk <= 8))
        def _():
            task_3(kk - 1)
        part_d(t, 0)
        part_b(t)

        @pl.when(kk >= 2)
        def _():
            task_4(kk - 2)
        t = 2 * kk + 1
        part_a(t)

        @pl.when(kk <= 7)
        def _():
            task_1(kk)
        part_d(t, 1)

        @pl.when(kk <= 7)
        def _():
            task_2(kk, 0, 4)
        part_b(t)

        @pl.when(kk <= 7)
        def _():
            task_2(kk, 4, 8)
        return carry

    lax.fori_loop(0, n // 2 + 2, pair_body, 0)
    for d in range(2):
        pair_copy(xb, sem_of(x_ps), sem_of(x_pr), n - 1, d).wait_send()
    pp_copy(n // 2 - 2).wait_send()
    pp_copy(n // 2 - 1).wait_send()
    for i in range(12, 15):
        local(i).start()

    for i in (7, 8, 9, 10, 11):
        local(i).wait()

    def norm(c, carry):
        rows = pl.ds(pl.multiple_of(c * 16, 16), 16)
        xf = xin[rows, :].astype(F32)
        inv = lax.rsqrt(jnp.mean(xf * xf, axis=-1, keepdims=True) + NORM_EPS)
        gx = (acc0[rows, :] + rs_recv[n % 3, rows, :].astype(F32)).astype(BF16)
        scaled = gx.astype(F32) * gamma[...].astype(F32)
        proj = jnp.mean(scaled * xf, axis=-1, keepdims=True)
        yb[0, rows, :] = (gr[rows, :].astype(F32) + inv * (scaled - xf * (inv * inv) * proj)).astype(BF16)
        return carry
    lax.fori_loop(0, tok // 16, norm, 0)
    local(15).start()

    def s_sem(arr, c):
        return lambda s, d: arr.at[d, c, s % 4]

    def o_task(m, c):
        cols = pl.ds(pl.multiple_of(c * ct, ct), ct)
        blk = yb[m % 3, :, cols]
        acc_o[:, cols] += dot(o_pair[...], blk, TN)
        part = dot(blk, wo[:, cols], NT)

        @pl.when(c == 0)
        def _():
            do_acc[...] = part

        @pl.when(c > 0)
        def _():
            do_acc[...] += part

    def o_rows(m):
        for i in range(2):
            for rel in range(2):
                for d in range(2):
                    yield i * 2 * tok + rel * tok + d * half, token_row(2 * m + i, rel, d)

    def o_begin(m):
        for r0, row in o_rows(m):
            o_pair[pl.ds(r0, half), :] = ov[pl.ds(row, half), :]

    def o_end(m):
        for r0, row in o_rows(m):
            do_v[pl.ds(row, half), :] = do_acc[pl.ds(r0, half), :].astype(BF16)

    def s_step(u, carry):
        m = u // 2 - 1

        @pl.when(u == 2)
        def _():
            local(15).wait()

        @pl.when(jnp.logical_and(u >= 2, u % 2 == 0))
        def _():
            o_begin(m)
        for c in range(SUBS):
            cols = pl.ds(c * sub_w, sub_w)
            rs, rr, ps, pr = (s_sem(a, c) for a in (s_rs, s_rr, s_ps, s_pr))
            for d in range(2):
                @pl.when(jnp.logical_and(u >= 2, u <= n + 1))
                def _():
                    pair_copy(yb, ps, pr, u - 2, d, cols).wait_send()

                @pl.when(jnp.logical_and(u >= 2, u <= n))
                def _():
                    ring_copy(yb, rs, rr, u - 2, d, cols).wait_send()

                @pl.when(jnp.logical_and(u >= 1, u <= n - 1))
                def _():
                    ring_copy(yb, rs, rr, u - 1, d, cols).wait_recv()

                @pl.when(u <= n - 2)
                def _():
                    ring_copy(yb, rs, rr, u, d, cols).start()

                @pl.when(u <= n - 1)
                def _():
                    pair_copy(yb, ps, pr, u, d, cols).start()

            @pl.when(u >= 2)
            def _():
                o_task(m, (u % 2) * SUBS + c)

        for c in range(SUBS):
            cols = pl.ds(c * sub_w, sub_w)
            for d in range(2):
                @pl.when(u <= n - 1)
                def _():
                    pair_copy(yb, s_sem(s_ps, c), s_sem(s_pr, c), u, d, cols).wait_recv()

        @pl.when(jnp.logical_and(u >= 2, u % 2 == 1))
        def _():
            o_end(m)
        return carry

    lax.fori_loop(0, n + 2, s_step, 0)
    local(16).start()
    local(17).start()
    for i in (12, 13, 14, 16, 17):
        local(i).wait()


def mega(side, *args):
    tok, hid = args[0].shape
    fl, rows = args[2].shape
    ol = args[10].shape[1]
    dma = pltpu.SemaphoreType.DMA
    ring = [dma((2, SLOTS)) for _ in range(8)] + [dma((2, SUBS, 4)) for _ in range(4)]
    sems = ring + [dma((2, 2)), dma((2, 3)), dma((2,)), dma((2,)), dma((18,))]
    out_shape = (
        jax.ShapeDtypeStruct((tok, hid), BF16), jax.ShapeDtypeStruct((rows, ol), BF16),
        jax.ShapeDtypeStruct((fl, hid), F32), jax.ShapeDtypeStruct((fl, hid), F32),
        jax.ShapeDtypeStruct((fl, hid), F32), jax.ShapeDtypeStruct((ol, hid), F32))
    v = pltpu.VMEM
    blk = 4 * tok
    scratch = [
        v((3, blk, hid), BF16), v((3, blk, hid), BF16), v((fl, rows), BF16), v((fl, rows), BF16), v((rows, fl), BF16), v((rows, fl), BF16),
        v((fl, hid), BF16), v((fl, hid), BF16), v((fl, hid), BF16), v((tok, hid), BF16), v((1, hid), BF16),
        v((tok, hid), BF16), v((rows, ol), BF16), v((ol, hid), BF16),
        v((fl, hid), F32), v((fl, hid), F32), v((fl, hid), F32), v((ol, hid), F32),
        v((blk, fl), F32), v((2, blk, fl), BF16), v((2, blk, fl), BF16), v((blk, fl), BF16),
        v((2, 2 * tok, hid), BF16), v((2, 2 * tok, hid), BF16), v((2, 2 * tok, hid), BF16),
        v((2, tok, hid), BF16), v((3, tok, hid), BF16), v((tok, hid), F32),
        v((rows, ol), BF16), v((blk, ol), F32), v((blk, ol), BF16)]
    anyspec = pl.BlockSpec(memory_space=pl.ANY)
    return pl.pallas_call(
        functools.partial(kernel, side),
        out_shape=out_shape,
        in_specs=[anyspec] * 12,
        out_specs=tuple([anyspec] * 6),
        scratch_shapes=scratch + sems,
        compiler_params=pltpu.CompilerParams(collective_id=0, has_side_effects=True, vmem_limit_bytes=67043328),
    )(*args)


def solution(mesh):
    token_spec = P(("dp", "tp"), None)
    split_cols = P("dp", "tp")
    weight_cols = P(None, "tp")
    weight_rows = P("tp", None)
    side = math.isqrt(mesh.shape["tp"] // 2)

    def local_backward(x_norm, grad_y, u_gate, u_up, w_gate, w_up, w_down, x_in, gamma, grad_res, attn_out, w_out):
        grad_sum, grad_attn, gw_gate, gw_up, gw_down, gw_out = mega(
            side, x_norm, grad_y, u_gate.T, u_up.T, w_gate.T, w_up.T, w_down, x_in, gamma.reshape(1, -1),
            grad_res, attn_out, w_out)
        return grad_sum, grad_attn, gw_gate.T, gw_up.T, gw_down, gw_out

    return jax.shard_map(
        local_backward,
        mesh=mesh,
        in_specs=(token_spec, token_spec, split_cols, split_cols, weight_cols, weight_cols, weight_rows,
                  token_spec, P(None), token_spec, split_cols, weight_rows),
        out_specs=(token_spec, split_cols, split_cols, split_cols, token_spec, token_spec),
        check_vma=False,
    )
```

time: 407 us -> 260 us (0.64)
  waiting for transfers between devices: 283 us -> 0 us
  Pallas kernels: 0 us -> 240 us
  matrix products: 104 us -> 0 us
  local copies, waits for them, and re-layouts: 1.89 us -> 19.3 us
  between operations: 13.9 us -> 0.65 us
    pallas_call x0 -> x1, Pallas kernels: none -> 240 us  [mega(): pl.pallas_call(functools.partial(kernel, side), out_shape=out_shape, in_s...]
    all_gather x3 -> x0, waiting for transfers between devices: 177 us -> none  [the longest x1 73.6 us: local_backward(): gy_full = lax.all_gather(grad_y, 'tp', axis=0, tiled=True)]
    reduce_scatter x1 -> x0, waiting for transfers between devices: 104 us -> none  [local_backward(): lax.psum_scatter(part_x.astype(jnp.bfloat16), 'tp', scatter_dimension=0,...]
    dot_general x8 -> x0, matrix products: 104 us -> none  [the longest x1 23.6 us: local_backward(): lax.dot_general(grad_up, w_up, CONTRACT_COLS, preferred_element_type=jnp....]
    unnamed x31 -> x14, local copies, waits for them, and re-layouts: 1.89 us -> 18 us
  transfers between devices with their start and end apart: 4 -> 0, of which waited for: 4 -> 0; matrix products, arithmetic and copies ran while one was open for 9% -> 0% of each run, Pallas kernels for 0% -> 0%
where the time goes in v1:
time: 260 us
  Pallas kernels  240 us (92%)
  local copies, waits for them, and re-layouts  19.3 us (7%)
    pallas_call x1, Pallas kernels, mega(): pl.pallas_call(functools.partial(kernel, side), out_shape=out_shape, in_s...  240 us
    unnamed x14, local copies, waits for them, and re-layouts  18 us

profile of v1, /device:TPU:97, one launch (start us, length us, event | category | flops | bytes accessed | tf_op | source)
XLA Modules:
  0.0 260.1 jit_solution(14039717936030709224)
XLA Ops:
  0.6 1.3 reshape.15.gamma_hbm
  1.9 240.1 %shard_map.163 = (bf16[64,4096]{1,0:T(8,128)(2,1)}, bf16[2048,128]{1,0:T(8,128)(2,1)}, f32[344,4096]{1,0:T(8,128)}, f32[344,4096]{1,0:T(8,128)}, f32[344,4096]{1,0:T(8,128)}, /*index=5*/f32[128,4096]{1,0:T(8,128)}) custom-call(bf16[64,4096]{1,0:T(8,128)(2,1)} %x_in_hbm.1, bf16[64,4096]{1,0:T(8,128)(2,1)} %gy_in_hbm.1, bf16[344,2048]{1,0:T(8,128)(2,1)} %bitcast.12, ...), custom_call_target="tpu_custom_call" | custom-call | tf_op jit(solution)/shard_map/pallas_call | solution.py:424
  242.0 1.9 copy.24
  243.9 1.9 copy.25
  245.8 0.0 copy-start
  245.8 0.0 slice-start
  245.8 6.2 %copy.26 = f32[4096,344]{0,1:T(8,128)} copy(f32[4096,344]{0,1:T(8,128)} %bitcast.9) | data formatting | bytes 11272192
  252.0 0.0 copy-done
  252.0 0.0 slice-start.1
  252.0 2.7 %copy.27 = f32[4096,344]{0,1:T(8,128)} copy(f32[4096,344]{0,1:T(8,128)S(1)} %bitcast.8) | data formatting | bytes 11272192
  254.8 0.0 slice-done
  254.8 0.9 slice-done.1
  255.6 0.0 copy-start.1
  255.6 2.6 %copy.28 = f32[344,4096]{1,0:T(8,128)} copy(f32[344,4096]{1,0:T(8,128)S(1)} %bitcast.7) | data formatting | bytes 11272192
  258.2 0.5 copy-done.1
  258.8 1.3 copy.29
  (1 shorter events, 0.0 us)
Async XLA Ops:
  245.8 6.2 %copy-start = (f32[344,4096]{1,0:T(8,128)S(1)}, f32[344,4096]{1,0:T(8,128)}, u32[]{:S(2)}) copy-start(f32[344,4096]{1,0:T(8,128)} %get-tuple-element.15) | copy-start | bytes 16908292
  245.8 9.0 %slice-start = ((s8[5636096]{0:T(1024)(128)(4,1)}), s8[4194304]{0:T(1024)(128)(4,1)S(1)}, s32[]{:S(2)}) async-start(s8[5636096]{0:T(1024)(128)(4,1)} %bitcast.6), calls=%async_computation | async-start | bytes 8388608
  252.0 3.6 %slice-start.1 = ((s8[5636096]{0:T(1024)(128)(4,1)}), s8[1441792]{0:T(1024)(128)(4,1)S(1)}, s32[]{:S(2)}) async-start(s8[5636096]{0:T(1024)(128)(4,1)} %bitcast.6), calls=%async_computation.1 | async-start | bytes 2883584
  255.6 3.1 %copy-start.1 = (f32[128,4096]{1,0:T(8,128)S(1)}, f32[128,4096]{1,0:T(8,128)}, u32[]{:S(2)}) copy-start(f32[128,4096]{1,0:T(8,128)} %get-tuple-element.29) | copy-start | bytes 6291460

commit v2 on v1

v2 whole, which is shorter than its diff:
```python
import functools
import math

import jax
import jax.numpy as jnp
from jax import lax
from jax.experimental import pallas as pl
from jax.experimental.pallas import tpu as pltpu
from jax.sharding import PartitionSpec as P

NORM_EPS = 1e-5
F32, BF16 = jnp.float32, jnp.bfloat16
LAG_X = 2
LAG_R = 2
PIECES = 2
SUBS = 4
SLOTS = 6
NN = (((1,), (0,)), ((), ()))
NT = (((1,), (1,)), ((), ()))
TN = (((0,), (0,)), ((), ()))


def dot(a, b, dims):
    return lax.dot_general(a, b, dims, preferred_element_type=F32)


def kernel(side, x_in_hbm, gy_in_hbm, ug_hbm, uu_hbm, wg_hbm, wu_hbm, wd_hbm, xin_hbm, gamma_hbm, gr_hbm, o_hbm, wo_hbm,
           ds_out, do_v, acc_g, acc_u, acc_d, acc_o,
           yb, xb, ugt, uut, ug, uu, wg, wu, wd, xin, gamma, gr, ov, wo,
           g_s, du_g, du_u, z_s, own_part, pp_send, pp_recv, rs_send, rs_recv, acc0,
           do_acc, o_pair,
           y_rs, y_rr, y_ps, y_pr, x_rs, x_rr, x_ps, x_pr,
           s_rs, s_rr, s_ps, s_pr, r_s, r_r, q_s, q_r, loc):
    n = side * side
    tok, hid = x_in_hbm.shape
    half = tok // 2
    ct = hid // 8

    me = lax.axis_index("tp")
    core = me % 2
    chip = me // 2
    cy, cx = chip // side, chip % side
    diag = (cx + cy) % side
    pos_own = side * (cy * (1 - core) + cx * core) + diag
    pos_par = side * (cx * (1 - core) + cy * core) + diag

    def index_of(e, q):
        a, b = q // side, q % side
        o = (b - a + side) % side
        yy = a * (1 - e) + o * e
        xx = o * (1 - e) + a * e
        return (yy * side + xx) * 2 + e

    partner = me + 1 - 2 * core
    nxt = (index_of(core, (pos_own + 1) % n), index_of(core, (pos_own + n - 1) % n))

    def token_row(s, rel, d):
        e = core if rel == 0 else 1 - core
        base = pos_own if rel == 0 else pos_par
        q = (base + n - s) % n if d == 0 else (base + s) % n
        return pl.multiple_of(index_of(e, q) * tok + half * d, half)

    def remote(src, dst, ssem, rsem, dev):
        return pltpu.make_async_remote_copy(src_ref=src, dst_ref=dst, send_sem=ssem, recv_sem=rsem,
                                            device_id={"tp": dev}, device_id_type=pl.DeviceIdType.MESH)

    def local(i):
        pairs = ((gy_in_hbm, yb.at[0, pl.ds(0, tok), :]), (x_in_hbm, xb.at[0, pl.ds(0, tok), :]),
                 (wd_hbm, wd), (ug_hbm, ugt), (uu_hbm, uut), (wg_hbm, wg), (wu_hbm, wu),
                 (xin_hbm, xin), (gamma_hbm, gamma), (gr_hbm, gr), (o_hbm, ov), (wo_hbm, wo))
        return pltpu.make_async_copy(pairs[i][0], pairs[i][1], loc.at[i])

    for i in range(12):
        local(i).start()

    barrier = pltpu.get_barrier_semaphore()
    for dev in (nxt[0], nxt[1], partner):
        pl.semaphore_signal(barrier, inc=1, device_id={"tp": dev}, device_id_type=pl.DeviceIdType.MESH)
    pl.semaphore_wait(barrier, 3)

    def rows_at(s, rel, d):
        return pl.ds(pl.multiple_of((s % 2) * (2 * tok) + rel * tok + d * half, half), half)

    def cols_of(c, pieces):
        return pl.ds(c * (hid // pieces), hid // pieces)

    def ring_copy(b, sems, s, d, c, pieces):
        cols = cols_of(c, pieces)
        m = sems[0].shape[2]
        return remote(b.at[(s // 2) % 3, rows_at(s, 0, d), cols], b.at[((s + 1) // 2) % 3, rows_at(s + 1, 0, d), cols],
                      sems[0].at[d, c, s % m], sems[1].at[d, c, (s + 1) % m], nxt[d])

    def pair_copy(b, sems, s, d, c, pieces):
        cols = cols_of(c, pieces)
        m = sems[0].shape[2]
        return remote(b.at[(s // 2) % 3, rows_at(s, 0, d), cols], b.at[(s // 2) % 3, rows_at(s, 1, d), cols],
                      sems[2].at[d, c, s % m], sems[3].at[d, c, s % m], partner)

    def between(s, lo, hi):
        return jnp.logical_and(s >= lo, s <= hi)

    def each(pieces, f):
        for c in range(pieces):
            for d in range(2):
                f(d, c, pieces)

    def forward(b, sems, s, first):
        @pl.when(s == 0)
        def _():
            local(first).wait()

        def one(d, c, pieces):
            @pl.when(between(s, 1, n - 1))
            def _():
                ring_copy(b, sems, s - 1, d, c, pieces).wait_recv()

            @pl.when(between(s, 0, n - 2))
            def _():
                ring_copy(b, sems, s, d, c, pieces).start()

            @pl.when(between(s, 0, n - 1))
            def _():
                pair_copy(b, sems, s, d, c, pieces).start()
        each(PIECES, one)

        @pl.when(between(s, 2, n + 1))
        def _():
            each(PIECES, lambda d, c, p: pair_copy(b, sems, s - 2, d, c, p).wait_send())

        @pl.when(between(s, 2, n))
        def _():
            each(PIECES, lambda d, c, p: ring_copy(b, sems, s - 2, d, c, p).wait_send())

    def pair_wait(b, sems, s):
        each(PIECES, lambda d, c, p: pair_copy(b, sems, s, d, c, p).wait_recv())

    y_sems, x_sems, s_sems = (y_rs, y_rr, y_ps, y_pr), (x_rs, x_rr, x_ps, x_pr), (s_rs, s_rr, s_ps, s_pr)

    def part_a(t):
        forward(yb, y_sems, t, 0)

    def part_b(t):
        forward(xb, x_sems, t - LAG_X, 1)

    def task_1(k):
        @pl.when(k == 0)
        def _():
            for i in (2, 3, 4):
                local(i).wait()

            def turn(c, carry):
                cols = pl.ds(pl.multiple_of(c * 128, 128), 128)
                ug[cols, :] = ugt[:, cols].astype(F32).T.astype(BF16)
                uu[cols, :] = uut[:, cols].astype(F32).T.astype(BF16)
                return carry
            lax.fori_loop(0, ug.shape[0] // 128, turn, 0)
        pair_wait(yb, y_sems, 2 * k)
        pair_wait(yb, y_sems, 2 * k + 1)
        g_s[...] = dot(wd[...], yb[k % 3], NT).T
        for i in range(2):
            for rel in range(2):
                for d in range(2):
                    r0 = i * 2 * tok + rel * tok + d * half
                    row = token_row(2 * k + i, rel, d)
                    gate = ug[pl.ds(row, half), :].astype(F32)
                    up = uu[pl.ds(row, half), :].astype(F32)
                    sig = jax.nn.sigmoid(gate)
                    act = gate * sig
                    grad = g_s[pl.ds(r0, half), :]
                    z_s[pl.ds(r0, half), :] = (act * up).astype(BF16)
                    du_u[k % 2, pl.ds(r0, half), :] = (grad * act).astype(BF16)
                    du_g[k % 2, pl.ds(r0, half), :] = (grad * up * (sig * (1.0 + gate * (1.0 - sig)))).astype(BF16)

    def pp_copy(k):
        return remote(pp_send.at[k % 2], pp_recv.at[k % 2], q_s.at[k % 2], q_r.at[k % 2], partner)

    def task_2(k, lo, hi):
        ks = k % 2
        if lo == 0:
            @pl.when(k == 0)
            def _():
                local(5).wait()
                local(6).wait()

            @pl.when(k >= 2)
            def _():
                pp_copy(k - 2).wait_send()

        def body(c, carry):
            cols = pl.ds(pl.multiple_of(c * ct, ct), ct)
            r = (dot(du_g[ks], wg[:, cols], NN) + dot(du_u[ks], wu[:, cols], NN)).astype(BF16)
            for i in range(2):
                own_part[ks, pl.ds(i * tok, tok), cols] = r[i * 2 * tok:i * 2 * tok + tok]
                pp_send[ks, pl.ds(i * tok, tok), cols] = r[i * 2 * tok + tok:(i + 1) * 2 * tok]
            return carry
        lax.fori_loop(lo, hi, body, 0)
        if hi == 8:
            pp_copy(k).start()

    def task_3(k):
        def body(c, carry):
            cols = pl.ds(pl.multiple_of(c * ct, ct), ct)
            acc_d[:, cols] += dot(z_s[...], yb[k % 3, :, cols], TN)
            return carry
        lax.fori_loop(0, 8, body, 0)

    def task_4(k, lo, hi):
        if lo == 0:
            pair_wait(xb, x_sems, 2 * k)
            pair_wait(xb, x_sems, 2 * k + 1)

        def body(c, carry):
            cols = pl.ds(pl.multiple_of(c * ct, ct), ct)
            xt = xb[k % 3, :, cols]
            acc_g[:, cols] += dot(du_g[k % 2], xt, TN)
            acc_u[:, cols] += dot(du_u[k % 2], xt, TN)
            return carry
        lax.fori_loop(lo, hi, body, 0)

    def rs_copy(j, d, c, pieces):
        rows, cols = pl.ds(d * half, half), cols_of(c, pieces)
        return remote(rs_send.at[j % 2, rows, cols], rs_recv.at[(j + 1) % 3, rows, cols],
                      r_s.at[d, c, j % 2], r_r.at[d, c, (j + 1) % 3], nxt[d])

    def part_d(t, i):
        j = t - LAG_R
        ks = (j // 2) % 2
        rows = pl.ds(i * tok, tok)
        if i == 0:
            @pl.when(between(j, 0, n - 2))
            def _():
                pp_copy(j // 2).wait_recv()

            @pl.when(j == 0)
            def _():
                acc0[...] = own_part[ks, rows, :].astype(F32) + pp_recv[ks, rows, :].astype(F32)

        @pl.when(between(j, 3, n + 1))
        def _():
            each(PIECES, lambda d, c, p: rs_copy(j - 2, d, c, p).wait_send())

        def one(d, c, pieces):
            dr = pl.ds(d * half, half)
            pr = pl.ds(i * tok + d * half, half)
            cols = cols_of(c, pieces)

            @pl.when(between(j, 2, n))
            def _():
                rs_copy(j - 1, d, c, pieces).wait_recv()

            @pl.when(j == 1)
            def _():
                rs_send[j % 2, dr, cols] = (own_part[ks, pr, cols].astype(F32)
                                            + pp_recv[ks, pr, cols].astype(F32)).astype(BF16)

            @pl.when(between(j, 2, n - 1))
            def _():
                rs_send[j % 2, dr, cols] = (own_part[ks, pr, cols].astype(F32) + pp_recv[ks, pr, cols].astype(F32)
                                            + rs_recv[j % 3, dr, cols].astype(F32)).astype(BF16)

            @pl.when(between(j, 1, n - 1))
            def _():
                rs_copy(j, d, c, pieces).start()
        each(PIECES, one)

    def pair_body(kk, carry):
        t = 2 * kk
        part_a(t)

        @pl.when(kk == 0)
        def _():
            acc_d[...] = jnp.zeros_like(acc_d)
            acc_g[...] = jnp.zeros_like(acc_g)
            acc_u[...] = jnp.zeros_like(acc_u)
            acc_o[...] = jnp.zeros_like(acc_o)

        @pl.when(kk >= 2)
        def _():
            task_4(kk - 2, 0, 4)
        part_d(t, 0)

        @pl.when(kk >= 2)
        def _():
            task_4(kk - 2, 4, 8)
        part_b(t)
        t = 2 * kk + 1
        part_a(t)

        @pl.when(between(kk, 1, n // 2))
        def _():
            task_3(kk - 1)

        @pl.when(kk < n // 2)
        def _():
            task_1(kk)
        part_d(t, 1)

        @pl.when(kk < n // 2)
        def _():
            task_2(kk, 0, 4)
        part_b(t)

        @pl.when(kk < n // 2)
        def _():
            task_2(kk, 4, 8)
        return carry

    lax.fori_loop(0, n // 2 + 2, pair_body, 0)
    pp_copy(n // 2 - 2).wait_send()
    pp_copy(n // 2 - 1).wait_send()

    for i in (7, 8, 9, 10, 11):
        local(i).wait()

    def norm(c, carry):
        rows = pl.ds(pl.multiple_of(c * 16, 16), 16)
        xf = xin[rows, :].astype(F32)
        inv = lax.rsqrt(jnp.mean(xf * xf, axis=-1, keepdims=True) + NORM_EPS)
        gx = (acc0[rows, :] + rs_recv[n % 3, rows, :].astype(F32)).astype(BF16)
        scaled = gx.astype(F32) * gamma[...].astype(F32)
        proj = jnp.mean(scaled * xf, axis=-1, keepdims=True)
        ds = (gr[rows, :].astype(F32) + inv * (scaled - xf * (inv * inv) * proj)).astype(BF16)
        yb[0, rows, :] = ds
        ds_out[rows, :] = ds
        return carry
    lax.fori_loop(0, tok // 16, norm, 0)

    def o_task(m, c):
        cols = pl.ds(pl.multiple_of(c * ct, ct), ct)
        blk = yb[m % 3, :, cols]
        acc_o[:, cols] += dot(o_pair[...], blk, TN)
        part = dot(blk, wo[:, cols], NT)

        @pl.when(c == 0)
        def _():
            do_acc[...] = part

        @pl.when(c > 0)
        def _():
            do_acc[...] += part

    def o_rows(m):
        for i in range(2):
            for rel in range(2):
                for d in range(2):
                    yield i * 2 * tok + rel * tok + d * half, token_row(2 * m + i, rel, d)

    def o_begin(m):
        for r0, row in o_rows(m):
            o_pair[pl.ds(r0, half), :] = ov[pl.ds(row, half), :]

    def o_end(m):
        for r0, row in o_rows(m):
            do_v[pl.ds(row, half), :] = do_acc[pl.ds(r0, half), :].astype(BF16)

    def s_step(u, carry):
        m = u // 2 - 1

        @pl.when(jnp.logical_and(u >= 2, u % 2 == 0))
        def _():
            each(SUBS, lambda d, c, p: pair_copy(yb, s_sems, 2 * m, d, c, p).wait_recv())
            each(SUBS, lambda d, c, p: pair_copy(yb, s_sems, 2 * m + 1, d, c, p).wait_recv())
            o_begin(m)
        for c in range(SUBS):
            for d in range(2):
                @pl.when(between(u, 1, n - 1))
                def _():
                    ring_copy(yb, s_sems, u - 1, d, c, SUBS).wait_recv()

                @pl.when(u <= n - 2)
                def _():
                    ring_copy(yb, s_sems, u, d, c, SUBS).start()

                @pl.when(u <= n - 1)
                def _():
                    pair_copy(yb, s_sems, u, d, c, SUBS).start()

                @pl.when(between(u, 2, n + 1))
                def _():
                    pair_copy(yb, s_sems, u - 2, d, c, SUBS).wait_send()

                @pl.when(between(u, 2, n))
                def _():
                    ring_copy(yb, s_sems, u - 2, d, c, SUBS).wait_send()

            @pl.when(u >= 2)
            def _():
                o_task(m, (u % 2) * SUBS + c)

        @pl.when(jnp.logical_and(u >= 2, u % 2 == 1))
        def _():
            o_end(m)
        return carry

    lax.fori_loop(0, n + 2, s_step, 0)


def mega(side, *args):
    tok, hid = args[0].shape
    fl, rows = args[2].shape
    ol = args[10].shape[1]
    dma = pltpu.SemaphoreType.DMA
    ring = [dma((2, PIECES, SLOTS)) for _ in range(8)] + [dma((2, SUBS, 4)) for _ in range(4)]
    sems = ring + [dma((2, PIECES, 2)), dma((2, PIECES, 3)), dma((2,)), dma((2,)), dma((12,))]
    out_shape = (pltpu.VMEM((tok, hid), BF16), pltpu.VMEM((rows, ol), BF16), pltpu.VMEM((fl, hid), F32),
                 pltpu.VMEM((fl, hid), F32), pltpu.VMEM((fl, hid), F32), pltpu.VMEM((ol, hid), F32))
    v = pltpu.VMEM
    blk = 4 * tok
    scratch = [
        v((3, blk, hid), BF16), v((3, blk, hid), BF16), v((fl, rows), BF16), v((fl, rows), BF16), v((rows, fl), BF16), v((rows, fl), BF16),
        v((fl, hid), BF16), v((fl, hid), BF16), v((fl, hid), BF16), v((tok, hid), BF16), v((1, hid), BF16),
        v((tok, hid), BF16), v((rows, ol), BF16), v((ol, hid), BF16),
        v((blk, fl), F32), v((2, blk, fl), BF16), v((2, blk, fl), BF16), v((blk, fl), BF16),
        v((2, 2 * tok, hid), BF16), v((2, 2 * tok, hid), BF16), v((2, 2 * tok, hid), BF16),
        v((2, tok, hid), BF16), v((3, tok, hid), BF16), v((tok, hid), F32),
        v((blk, ol), F32), v((blk, ol), BF16)]
    anyspec = pl.BlockSpec(memory_space=pl.ANY)
    return pl.pallas_call(
        functools.partial(kernel, side),
        out_shape=out_shape,
        in_specs=[anyspec] * 12,
        out_specs=tuple([pl.BlockSpec(memory_space=pltpu.VMEM)] * 6),
        scratch_shapes=scratch + sems,
        compiler_params=pltpu.CompilerParams(collective_id=0, has_side_effects=True, vmem_limit_bytes=45000000),
    )(*args)


def solution(mesh):
    token_spec = P(("dp", "tp"), None)
    split_cols = P("dp", "tp")
    weight_cols = P(None, "tp")
    weight_rows = P("tp", None)
    side = math.isqrt(mesh.shape["tp"] // 2)

    def local_backward(x_norm, grad_y, u_gate, u_up, w_gate, w_up, w_down, x_in, gamma, grad_res, attn_out, w_out):
        grad_sum, grad_attn, gw_gate, gw_up, gw_down, gw_out = mega(
            side, x_norm, grad_y, u_gate.T, u_up.T, w_gate.T, w_up.T, w_down, x_in, gamma.reshape(1, -1),
            grad_res, attn_out, w_out)
        return grad_sum, grad_attn, gw_gate.T, gw_up.T, gw_down, gw_out

    return jax.shard_map(
        local_backward,
        mesh=mesh,
        in_specs=(token_spec, token_spec, split_cols, split_cols, weight_cols, weight_cols, weight_rows,
                  token_spec, P(None), token_spec, split_cols, weight_rows),
        out_specs=(token_spec, split_cols, split_cols, split_cols, token_spec, token_spec),
        check_vma=False,
    )
```

time: 260 us -> 227 us (0.87)
  Pallas kernels: 240 us -> 214 us
  local copies, waits for them, and re-layouts: 19.3 us -> 11.7 us
    pallas_call x1, Pallas kernels: 240 us -> 214 us  [mega(): pl.pallas_call(functools.partial(kernel, side), out_shape=out_shape, in_s...]
    unnamed x14 -> x6, local copies, waits for them, and re-layouts: 18 us -> 10.4 us
where the time goes in v2:
time: 227 us
  Pallas kernels  214 us (94%)
  local copies, waits for them, and re-layouts  11.7 us (5%)
    pallas_call x1, Pallas kernels, mega(): pl.pallas_call(functools.partial(kernel, side), out_shape=out_shape, in_s...  214 us
    unnamed x6, local copies, waits for them, and re-layouts  10.4 us

profile of v2, /device:TPU:97, one launch (start us, length us, event | category | flops | bytes accessed | tf_op | source)
XLA Modules:
  0.0 226.8 jit_solution(1686465184553176857)
XLA Ops:
  0.6 1.3 reshape.15.gamma_hbm
  1.9 214.5 %shard_map.163 = (bf16[64,4096]{1,0:T(8,128)(2,1)S(1)}, bf16[2048,128]{1,0:T(8,128)(2,1)S(1)}, f32[344,4096]{1,0:T(8,128)S(1)}, f32[344,4096]{1,0:T(8,128)S(1)},...) custom-call(bf16[64,4096]{1,0:T(8,128)(2,1)} %x_in_hbm.1, bf16[64,4096]{1,0:T(8,128)(2,1)} %gy_in_hbm.1, ...), custom_call_target="tpu_custom_call" | custom-call | tf_op jit(solution)/shard_map/pallas_call | solution.py:418
  216.4 0.8 copy.24
  217.2 0.8 copy.25
  218.0 1.3 copy.29
  219.3 2.5 %copy.26 = f32[4096,344]{0,1:T(8,128)} copy(f32[4096,344]{0,1:T(8,128)S(1)} %bitcast.7) | data formatting | bytes 11272192
  221.8 2.5 %copy.27 = f32[4096,344]{0,1:T(8,128)} copy(f32[4096,344]{0,1:T(8,128)S(1)} %bitcast.6) | data formatting | bytes 11272192
  224.3 2.5 %copy.28 = f32[344,4096]{1,0:T(8,128)} copy(f32[344,4096]{1,0:T(8,128)S(1)} %get-tuple-element.22) | data formatting | bytes 11272192

commit v3 on v2

--- a/solution.py
+++ b/solution.py
@@ -10,9 +10,9 @@
 
 NORM_EPS = 1e-5
 F32, BF16 = jnp.float32, jnp.bfloat16
-LAG_X = 2
-LAG_R = 2
+LAG_R = 3
 PIECES = 2
+X_PIECES = 4
 SUBS = 4
 SLOTS = 6
 NN = (((1,), (0,)), ((), ()))
@@ -27,7 +27,7 @@
 def kernel(side, x_in_hbm, gy_in_hbm, ug_hbm, uu_hbm, wg_hbm, wu_hbm, wd_hbm, xin_hbm, gamma_hbm, gr_hbm, o_hbm, wo_hbm,
            ds_out, do_v, acc_g, acc_u, acc_d, acc_o,
            yb, xb, ugt, uut, ug, uu, wg, wu, wd, xin, gamma, gr, ov, wo,
-           g_s, du_g, du_u, z_s, own_part, pp_send, pp_recv, rs_send, rs_recv, acc0,
+           g_s, g_t, du_g, du_u, z_s, own_part, pp_send, pp_recv, rs_send, rs_recv, acc0,
            do_acc, o_pair,
            y_rs, y_rr, y_ps, y_pr, x_rs, x_rr, x_ps, x_pr,
            s_rs, s_rr, s_ps, s_pr, r_s, r_r, q_s, q_r, loc):
@@ -99,15 +99,12 @@
     def between(s, lo, hi):
         return jnp.logical_and(s >= lo, s <= hi)
 
-    def each(pieces, f):
-        for c in range(pieces):
+    def each(pieces, f, part=None):
+        for c in part or range(pieces):
             for d in range(2):
                 f(d, c, pieces)
 
-    def forward(b, sems, s, first):
-        @pl.when(s == 0)
-        def _():
-            local(first).wait()
+    def forward(b, sems, s, pieces, part=None):
 
         def one(d, c, pieces):
             @pl.when(between(s, 1, n - 1))
@@ -121,26 +118,37 @@
             @pl.when(between(s, 0, n - 1))
             def _():
                 pair_copy(b, sems, s, d, c, pieces).start()
-        each(PIECES, one)
+        each(pieces, one, part)
 
         @pl.when(between(s, 2, n + 1))
         def _():
-            each(PIECES, lambda d, c, p: pair_copy(b, sems, s - 2, d, c, p).wait_send())
+            each(pieces, lambda d, c, p: pair_copy(b, sems, s - 2, d, c, p).wait_send(), part)
 
         @pl.when(between(s, 2, n))
         def _():
-            each(PIECES, lambda d, c, p: ring_copy(b, sems, s - 2, d, c, p).wait_send())
-
-    def pair_wait(b, sems, s):
-        each(PIECES, lambda d, c, p: pair_copy(b, sems, s, d, c, p).wait_recv())
+            each(pieces, lambda d, c, p: ring_copy(b, sems, s - 2, d, c, p).wait_send(), part)
+
+    def pair_wait(b, sems, s, pieces, part=None):
+        each(pieces, lambda d, c, p: pair_copy(b, sems, s, d, c, p).wait_recv(), part)
 
     y_sems, x_sems, s_sems = (y_rs, y_rr, y_ps, y_pr), (x_rs, x_rr, x_ps, x_pr), (s_rs, s_rr, s_ps, s_pr)
 
+    early, late = tuple(range(X_PIECES // 2)), tuple(range(X_PIECES // 2, X_PIECES))
+
     def part_a(t):
-        forward(yb, y_sems, t, 0)
+        @pl.when(t == 0)
+        def _():
+            local(0).wait()
+        forward(yb, y_sems, t, PIECES)
 
     def part_b(t):
-        forward(xb, x_sems, t - LAG_X, 1)
+        @pl.when(t == 0)
+        def _():
+            local(1).wait()
+        forward(xb, x_sems, t, X_PIECES, early)
+
+    def part_c(s):
+        forward(xb, x_sems, s, X_PIECES, late)
 
     def task_1(k):
         @pl.when(k == 0)
@@ -154,9 +162,12 @@
                 uu[cols, :] = uut[:, cols].astype(F32).T.astype(BF16)
                 return carry
             lax.fori_loop(0, ug.shape[0] // 128, turn, 0)
-        pair_wait(yb, y_sems, 2 * k)
-        pair_wait(yb, y_sems, 2 * k + 1)
-        g_s[...] = dot(wd[...], yb[k % 3], NT).T
+        pair_wait(yb, y_sems, 2 * k, PIECES)
+        pair_wait(yb, y_sems, 2 * k + 1, PIECES)
+        g_t[...] = dot(wd[:, :hid // 2], yb[k % 3, :, :hid // 2], NT)
+
+    def task_1b(k):
+        g_s[...] = (g_t[...] + dot(wd[:, hid // 2:], yb[k % 3, :, hid // 2:], NT)).T
         for i in range(2):
             for rel in range(2):
                 for d in range(2):
@@ -168,8 +179,8 @@
                     act = gate * sig
                     grad = g_s[pl.ds(r0, half), :]
                     z_s[pl.ds(r0, half), :] = (act * up).astype(BF16)
-                    du_u[k % 2, pl.ds(r0, half), :] = (grad * act).astype(BF16)
-                    du_g[k % 2, pl.ds(r0, half), :] = (grad * up * (sig * (1.0 + gate * (1.0 - sig)))).astype(BF16)
+                    du_u[k, pl.ds(r0, half), :] = (grad * act).astype(BF16)
+                    du_g[k, pl.ds(r0, half), :] = (grad * up * (sig * (1.0 + gate * (1.0 - sig)))).astype(BF16)
 
     def pp_copy(k):
         return remote(pp_send.at[k % 2], pp_recv.at[k % 2], q_s.at[k % 2], q_r.at[k % 2], partner)
@@ -188,7 +199,7 @@
 
         def body(c, carry):
             cols = pl.ds(pl.multiple_of(c * ct, ct), ct)
-            r = (dot(du_g[ks], wg[:, cols], NN) + dot(du_u[ks], wu[:, cols], NN)).astype(BF16)
+            r = (dot(du_g[k], wg[:, cols], NN) + dot(du_u[k], wu[:, cols], NN)).astype(BF16)
             for i in range(2):
                 own_part[ks, pl.ds(i * tok, tok), cols] = r[i * 2 * tok:i * 2 * tok + tok]
                 pp_send[ks, pl.ds(i * tok, tok), cols] = r[i * 2 * tok + tok:(i + 1) * 2 * tok]
@@ -205,15 +216,16 @@
         lax.fori_loop(0, 8, body, 0)
 
     def task_4(k, lo, hi):
-        if lo == 0:
-            pair_wait(xb, x_sems, 2 * k)
-            pair_wait(xb, x_sems, 2 * k + 1)
+        if lo in (0, 4):
+            part = early if lo == 0 else late
+            pair_wait(xb, x_sems, 2 * k, X_PIECES, part)
+            pair_wait(xb, x_sems, 2 * k + 1, X_PIECES, part)
 
         def body(c, carry):
             cols = pl.ds(pl.multiple_of(c * ct, ct), ct)
             xt = xb[k % 3, :, cols]
-            acc_g[:, cols] += dot(du_g[k % 2], xt, TN)
-            acc_u[:, cols] += dot(du_u[k % 2], xt, TN)
+            acc_g[:, cols] += dot(du_g[k], xt, TN)
+            acc_u[:, cols] += dot(du_u[k], xt, TN)
             return carry
         lax.fori_loop(lo, hi, body, 0)
 
@@ -269,45 +281,49 @@
 
         @pl.when(kk == 0)
         def _():
+            part_b(t)
             acc_d[...] = jnp.zeros_like(acc_d)
             acc_g[...] = jnp.zeros_like(acc_g)
             acc_u[...] = jnp.zeros_like(acc_u)
             acc_o[...] = jnp.zeros_like(acc_o)
 
-        @pl.when(kk >= 2)
-        def _():
-            task_4(kk - 2, 0, 4)
-        part_d(t, 0)
-
-        @pl.when(kk >= 2)
-        def _():
-            task_4(kk - 2, 4, 8)
-        part_b(t)
+        @pl.when(kk >= 1)
+        def _():
+            task_2(kk - 1, 0, 4)
+            part_d(t, 1)
+            task_2(kk - 1, 4, 8)
+            part_b(t)
+            task_4(kk - 1, 0, 4)
+
+        @pl.when(kk == n // 2)
+        def _():
+            part_c(t - n)
         t = 2 * kk + 1
         part_a(t)
 
-        @pl.when(between(kk, 1, n // 2))
+        @pl.when(kk >= 1)
         def _():
             task_3(kk - 1)
+            part_d(t, 0)
 
         @pl.when(kk < n // 2)
         def _():
             task_1(kk)
-        part_d(t, 1)
+        part_b(t)
 
         @pl.when(kk < n // 2)
         def _():
-            task_2(kk, 0, 4)
-        part_b(t)
-
-        @pl.when(kk < n // 2)
-        def _():
-            task_2(kk, 4, 8)
+            task_1b(kk)
+
+        @pl.when(kk == n // 2)
+        def _():
+            part_c(t - n)
         return carry
 
-    lax.fori_loop(0, n // 2 + 2, pair_body, 0)
-    pp_copy(n // 2 - 2).wait_send()
-    pp_copy(n // 2 - 1).wait_send()
+    lax.fori_loop(0, n // 2 + 1, pair_body, 0)
+    part_d(jnp.int32(n + 2), 1)
+    part_c(jnp.int32(2))
+    part_d(jnp.int32(n + 3), 0)
 
     for i in (7, 8, 9, 10, 11):
         local(i).wait()
@@ -317,7 +333,7 @@
         xf = xin[rows, :].astype(F32)
         inv = lax.rsqrt(jnp.mean(xf * xf, axis=-1, keepdims=True) + NORM_EPS)
         gx = (acc0[rows, :] + rs_recv[n % 3, rows, :].astype(F32)).astype(BF16)
-        scaled = gx.astype(F32) * gamma[...].astype(F32)
+        scaled = gx.astype(F32) * gamma[...].astype(F32).reshape(1, hid)
         proj = jnp.mean(scaled * xf, axis=-1, keepdims=True)
         ds = (gr[rows, :].astype(F32) + inv * (scaled - xf * (inv * inv) * proj)).astype(BF16)
         yb[0, rows, :] = ds
@@ -383,6 +399,9 @@
                 def _():
                     ring_copy(yb, s_sems, u - 2, d, c, SUBS).wait_send()
 
+            if c % 2 == 1:
+                forward(xb, x_sems, u + 3, X_PIECES, (late[c // 2],))
+
             @pl.when(u >= 2)
             def _():
                 o_task(m, (u % 2) * SUBS + c)
@@ -390,9 +409,24 @@
         @pl.when(jnp.logical_and(u >= 2, u % 2 == 1))
         def _():
             o_end(m)
+
+        @pl.when(u == 0)
+        def _():
+            task_4(0, 4, 8)
+
+        @pl.when(jnp.logical_and(u <= n - 2, u % 2 == 1))
+        def _():
+            task_4((u + 1) // 2, 4, 6)
+
+        @pl.when(jnp.logical_and(between(u, 2, n - 2), u % 2 == 0))
+        def _():
+            task_4(u // 2, 6, 8)
         return carry
 
     lax.fori_loop(0, n + 2, s_step, 0)
+    each(PIECES, lambda d, c, p: rs_copy(n - 1, d, c, p).wait_send())
+    pp_copy(n // 2 - 2).wait_send()
+    pp_copy(n // 2 - 1).wait_send()
 
 
 def mega(side, *args):
@@ -400,7 +434,7 @@
     fl, rows = args[2].shape
     ol = args[10].shape[1]
     dma = pltpu.SemaphoreType.DMA
-    ring = [dma((2, PIECES, SLOTS)) for _ in range(8)] + [dma((2, SUBS, 4)) for _ in range(4)]
+    ring = [dma((2, PIECES, SLOTS)) for _ in range(4)] + [dma((2, X_PIECES, SLOTS)) for _ in range(4)] + [dma((2, SUBS, 4)) for _ in range(4)]
     sems = ring + [dma((2, PIECES, 2)), dma((2, PIECES, 3)), dma((2,)), dma((2,)), dma((12,))]
     out_shape = (pltpu.VMEM((tok, hid), BF16), pltpu.VMEM((rows, ol), BF16), pltpu.VMEM((fl, hid), F32),
                  pltpu.VMEM((fl, hid), F32), pltpu.VMEM((fl, hid), F32), pltpu.VMEM((ol, hid), F32))
@@ -408,9 +442,9 @@
     blk = 4 * tok
     scratch = [
         v((3, blk, hid), BF16), v((3, blk, hid), BF16), v((fl, rows), BF16), v((fl, rows), BF16), v((rows, fl), BF16), v((rows, fl), BF16),
-        v((fl, hid), BF16), v((fl, hid), BF16), v((fl, hid), BF16), v((tok, hid), BF16), v((1, hid), BF16),
+        v((fl, hid), BF16), v((fl, hid), BF16), v((fl, hid), BF16), v((tok, hid), BF16), v((hid,), BF16),
         v((tok, hid), BF16), v((rows, ol), BF16), v((ol, hid), BF16),
-        v((blk, fl), F32), v((2, blk, fl), BF16), v((2, blk, fl), BF16), v((blk, fl), BF16),
+        v((blk, fl), F32), v((fl, blk), F32), v((rows // blk, blk, fl), BF16), v((rows // blk, blk, fl), BF16), v((blk, fl), BF16),
         v((2, 2 * tok, hid), BF16), v((2, 2 * tok, hid), BF16), v((2, 2 * tok, hid), BF16),
         v((2, tok, hid), BF16), v((3, tok, hid), BF16), v((tok, hid), F32),
         v((blk, ol), F32), v((blk, ol), BF16)]
@@ -421,8 +455,28 @@
         in_specs=[anyspec] * 12,
         out_specs=tuple([pl.BlockSpec(memory_space=pltpu.VMEM)] * 6),
         scratch_shapes=scratch + sems,
-        compiler_params=pltpu.CompilerParams(collective_id=0, has_side_effects=True, vmem_limit_bytes=45000000),
+        compiler_params=pltpu.CompilerParams(collective_id=0, has_side_effects=True, vmem_limit_bytes=46800000),
     )(*args)
+
+
+def flush_kernel(*refs):
+    k = len(refs) // 2
+    copies = [pltpu.make_async_copy(refs[i], refs[k + i], refs[-1].at[i]) for i in range(k)]
+    for c in copies:
+        c.start()
+    for c in copies:
+        c.wait()
+
+
+def flush(*arrays):
+    return pl.pallas_call(
+        flush_kernel,
+        out_shape=tuple(pltpu.HBM(a.shape, a.dtype) for a in arrays),
+        in_specs=[pl.BlockSpec(memory_space=pltpu.VMEM)] * len(arrays),
+        out_specs=tuple([pl.BlockSpec(memory_space=pltpu.HBM)] * len(arrays)),
+        scratch_shapes=[pltpu.SemaphoreType.DMA((len(arrays),))],
+        compiler_params=pltpu.CompilerParams(vmem_limit_bytes=1000000),
+    )(*[pltpu.with_memory_space_constraint(a, pltpu.VMEM) for a in arrays])
 
 
 def solution(mesh):
@@ -433,9 +487,9 @@
     side = math.isqrt(mesh.shape["tp"] // 2)
 
     def local_backward(x_norm, grad_y, u_gate, u_up, w_gate, w_up, w_down, x_in, gamma, grad_res, attn_out, w_out):
-        grad_sum, grad_attn, gw_gate, gw_up, gw_down, gw_out = mega(
-            side, x_norm, grad_y, u_gate.T, u_up.T, w_gate.T, w_up.T, w_down, x_in, gamma.reshape(1, -1),
-            grad_res, attn_out, w_out)
+        grad_sum, grad_attn, gw_gate, gw_up, gw_down, gw_out = flush(*mega(
+            side, x_norm, grad_y, u_gate.T, u_up.T, w_gate.T, w_up.T, w_down, x_in, gamma,
+            grad_res, attn_out, w_out))
         return grad_sum, grad_attn, gw_gate.T, gw_up.T, gw_down, gw_out
 
     return jax.shard_map(

time: 227 us -> 213 us (0.938)
  local copies, waits for them, and re-layouts: 11.7 us -> 0 us
    unnamed x6 -> x0, local copies, waits for them, and re-layouts: 10.4 us -> none
    pallas_call x1, Pallas kernels: 214 us -> 206 us  [mega(): pl.pallas_call(functools.partial(kernel, side), out_shape=out_shape, in_s...]
    pallas_call x0 -> x1, Pallas kernels: none -> 6.96 us  [flush(): pl.pallas_call(flush_kernel, out_shape=tuple((pltpu.HBM(a.shape, a.dtype)...]
where the time goes in v3:
time: 213 us
  Pallas kernels  213 us (100%)
    pallas_call x1, Pallas kernels, mega(): pl.pallas_call(functools.partial(kernel, side), out_shape=out_shape, in_s...  206 us
    pallas_call x1, Pallas kernels, flush(): pl.pallas_call(flush_kernel, out_shape=tuple((pltpu.HBM(a.shape, a.dtype)...  6.96 us

profile of v3, /device:TPU:97, one launch (start us, length us, event | category | flops | bytes accessed | tf_op | source)
XLA Modules:
  0.0 213.4 jit_solution(867603169141492096)
XLA Ops:
  0.6 205.8 %shard_map.163 = (bf16[64,4096]{1,0:T(8,128)(2,1)S(1)}, bf16[2048,128]{1,0:T(8,128)(2,1)S(1)}, f32[344,4096]{1,0:T(8,128)S(1)}, f32[344,4096]{1,0:T(8,128)S(1)},...) custom-call(bf16[64,4096]{1,0:T(8,128)(2,1)} %x_in_hbm.1, bf16[64,4096]{1,0:T(8,128)(2,1)} %gy_in_hbm.1, ...), custom_call_target="tpu_custom_call" | custom-call | tf_op jit(solution)/shard_map/pallas_call | solution.py:452
  206.4 7.0 %shard_map.164 = (bf16[64,4096]{1,0:T(8,128)(2,1)}, bf16[2048,128]{1,0:T(8,128)(2,1)}, f32[344,4096]{1,0:T(8,128)}, f32[344,4096]{1,0:T(8,128)}, f32[344,4096]{1,0:T(8,128)}, /*index=5*/f32[128,4096]{1,0:T(8,128)}) custom-call(bf16[64,4096]{1,0:T(8,128)(2,1)S(1)} %get-tuple-element.18.refs_0_, bf16[2048,128]{1,0:T(8,128)(2,1)S(1)} %get-tuple-element.19.refs_1_, ...), custom_call_target="tpu_custom_call" | custom-call | tf_op jit(solution)/shard_map/pallas_call | solution.py:472

commit v4 on v3

--- a/solution.py
+++ b/solution.py
@@ -13,6 +13,7 @@
 LAG_R = 3
 PIECES = 2
 X_PIECES = 4
+TILES = 4
 SUBS = 4
 SLOTS = 6
 NN = (((1,), (0,)), ((), ()))
@@ -27,14 +28,14 @@
 def kernel(side, x_in_hbm, gy_in_hbm, ug_hbm, uu_hbm, wg_hbm, wu_hbm, wd_hbm, xin_hbm, gamma_hbm, gr_hbm, o_hbm, wo_hbm,
            ds_out, do_v, acc_g, acc_u, acc_d, acc_o,
            yb, xb, ugt, uut, ug, uu, wg, wu, wd, xin, gamma, gr, ov, wo,
-           g_s, g_t, du_g, du_u, z_s, own_part, pp_send, pp_recv, rs_send, rs_recv, acc0,
+           g_s, du_g, du_u, z_s, own_part, pp_send, pp_recv, rs_send, rs_recv, acc0,
            do_acc, o_pair,
            y_rs, y_rr, y_ps, y_pr, x_rs, x_rr, x_ps, x_pr,
            s_rs, s_rr, s_ps, s_pr, r_s, r_r, q_s, q_r, loc):
     n = side * side
     tok, hid = x_in_hbm.shape
     half = tok // 2
-    ct = hid // 8
+    ct = hid // TILES
 
     me = lax.axis_index("tp")
     core = me % 2
@@ -164,10 +165,9 @@
             lax.fori_loop(0, ug.shape[0] // 128, turn, 0)
         pair_wait(yb, y_sems, 2 * k, PIECES)
         pair_wait(yb, y_sems, 2 * k + 1, PIECES)
-        g_t[...] = dot(wd[:, :hid // 2], yb[k % 3, :, :hid // 2], NT)
 
     def task_1b(k):
-        g_s[...] = (g_t[...] + dot(wd[:, hid // 2:], yb[k % 3, :, hid // 2:], NT)).T
+        g_s[...] = dot(wd[...], yb[k % 3], NT).T
         for i in range(2):
             for rel in range(2):
                 for d in range(2):
@@ -205,7 +205,7 @@
                 pp_send[ks, pl.ds(i * tok, tok), cols] = r[i * 2 * tok + tok:(i + 1) * 2 * tok]
             return carry
         lax.fori_loop(lo, hi, body, 0)
-        if hi == 8:
+        if hi == TILES:
             pp_copy(k).start()
 
     def task_3(k):
@@ -213,10 +213,10 @@
             cols = pl.ds(pl.multiple_of(c * ct, ct), ct)
             acc_d[:, cols] += dot(z_s[...], yb[k % 3, :, cols], TN)
             return carry
-        lax.fori_loop(0, 8, body, 0)
+        lax.fori_loop(0, TILES, body, 0)
 
     def task_4(k, lo, hi):
-        if lo in (0, 4):
+        if lo in (0, TILES // 2):
             part = early if lo == 0 else late
             pair_wait(xb, x_sems, 2 * k, X_PIECES, part)
             pair_wait(xb, x_sems, 2 * k + 1, X_PIECES, part)
@@ -289,11 +289,11 @@
 
         @pl.when(kk >= 1)
         def _():
-            task_2(kk - 1, 0, 4)
+            task_2(kk - 1, 0, TILES // 2)
             part_d(t, 1)
-            task_2(kk - 1, 4, 8)
+            task_2(kk - 1, TILES // 2, TILES)
             part_b(t)
-            task_4(kk - 1, 0, 4)
+            task_4(kk - 1, 0, TILES // 2)
 
         @pl.when(kk == n // 2)
         def _():
@@ -402,9 +402,10 @@
             if c % 2 == 1:
                 forward(xb, x_sems, u + 3, X_PIECES, (late[c // 2],))
 
-            @pl.when(u >= 2)
-            def _():
-                o_task(m, (u % 2) * SUBS + c)
+            if c % (2 * SUBS // TILES) == 0:
+                @pl.when(u >= 2)
+                def _():
+                    o_task(m, (u % 2) * (TILES // 2) + c * TILES // (2 * SUBS))
 
         @pl.when(jnp.logical_and(u >= 2, u % 2 == 1))
         def _():
@@ -412,15 +413,12 @@
 
         @pl.when(u == 0)
         def _():
-            task_4(0, 4, 8)
+            task_4(0, TILES // 2, TILES)
 
         @pl.when(jnp.logical_and(u <= n - 2, u % 2 == 1))
         def _():
-            task_4((u + 1) // 2, 4, 6)
-
-        @pl.when(jnp.logical_and(between(u, 2, n - 2), u % 2 == 0))
-        def _():
-            task_4(u // 2, 6, 8)
+            task_4((u + 1) // 2, TILES // 2, TILES)
+
         return carry
 
     lax.fori_loop(0, n + 2, s_step, 0)
@@ -444,7 +442,7 @@
         v((3, blk, hid), BF16), v((3, blk, hid), BF16), v((fl, rows), BF16), v((fl, rows), BF16), v((rows, fl), BF16), v((rows, fl), BF16),
         v((fl, hid), BF16), v((fl, hid), BF16), v((fl, hid), BF16), v((tok, hid), BF16), v((hid,), BF16),
         v((tok, hid), BF16), v((rows, ol), BF16), v((ol, hid), BF16),
-        v((blk, fl), F32), v((fl, blk), F32), v((rows // blk, blk, fl), BF16), v((rows // blk, blk, fl), BF16), v((blk, fl), BF16),
+        v((blk, fl), F32), v((rows // blk, blk, fl), BF16), v((rows // blk, blk, fl), BF16), v((blk, fl), BF16),
         v((2, 2 * tok, hid), BF16), v((2, 2 * tok, hid), BF16), v((2, 2 * tok, hid), BF16),
         v((2, tok, hid), BF16), v((3, tok, hid), BF16), v((tok, hid), F32),
         v((blk, ol), F32), v((blk, ol), BF16)]

time: 213 us -> 210 us (0.986)
  Pallas kernels: 213 us -> 209 us
    pallas_call x1, Pallas kernels: 206 us -> 202 us  [mega(): pl.pallas_call(functools.partial(kernel, side), out_shape=out_shape, in_s...]
where the time goes in v4:
time: 210 us
  Pallas kernels  209 us (100%)
    pallas_call x1, Pallas kernels, mega(): pl.pallas_call(functools.partial(kernel, side), out_shape=out_shape, in_s...  202 us
    pallas_call x1, Pallas kernels, flush(): pl.pallas_call(flush_kernel, out_shape=tuple((pltpu.HBM(a.shape, a.dtype)...  6.96 us

profile of v4, /device:TPU:97, one launch (start us, length us, event | category | flops | bytes accessed | tf_op | source)
XLA Modules:
  0.0 209.7 jit_solution(17742304898262833550)
XLA Ops:
  0.6 202.0 %shard_map.163 = (bf16[64,4096]{1,0:T(8,128)(2,1)S(1)}, bf16[2048,128]{1,0:T(8,128)(2,1)S(1)}, f32[344,4096]{1,0:T(8,128)S(1)}, f32[344,4096]{1,0:T(8,128)S(1)},...) custom-call(bf16[64,4096]{1,0:T(8,128)(2,1)} %x_in_hbm.1, bf16[64,4096]{1,0:T(8,128)(2,1)} %gy_in_hbm.1, ...), custom_call_target="tpu_custom_call" | custom-call | tf_op jit(solution)/shard_map/pallas_call | solution.py:450
  202.7 7.0 %shard_map.164 = (bf16[64,4096]{1,0:T(8,128)(2,1)}, bf16[2048,128]{1,0:T(8,128)(2,1)}, f32[344,4096]{1,0:T(8,128)}, f32[344,4096]{1,0:T(8,128)}, f32[344,4096]{1,0:T(8,128)}, /*index=5*/f32[128,4096]{1,0:T(8,128)}) custom-call(bf16[64,4096]{1,0:T(8,128)(2,1)S(1)} %get-tuple-element.18.refs_0_, bf16[2048,128]{1,0:T(8,128)(2,1)S(1)} %get-tuple-element.19.refs_1_, ...), custom_call_target="tpu_custom_call" | custom-call | tf_op jit(solution)/shard_map/pallas_call | solution.py:470

commit v5 on v4

--- a/solution.py
+++ b/solution.py
@@ -15,6 +15,8 @@
 X_PIECES = 4
 TILES = 4
 SUBS = 4
+MEGA_VMEM = 39000000
+FLUSH_VMEM = 4000000
 SLOTS = 6
 NN = (((1,), (0,)), ((), ()))
 NT = (((1,), (1,)), ((), ()))
@@ -25,9 +27,35 @@
     return lax.dot_general(a, b, dims, preferred_element_type=F32)
 
 
+def places(side, tok):
+    n, half = side * side, tok // 2
+    me = lax.axis_index("tp")
+    core = me % 2
+    chip = me // 2
+    cy, cx = chip // side, chip % side
+    diag = (cx + cy) % side
+    pos_own = side * (cy * (1 - core) + cx * core) + diag
+    pos_par = side * (cx * (1 - core) + cy * core) + diag
+
+    def index_of(e, q):
+        a, b = q // side, q % side
+        o = (b - a + side) % side
+        yy = a * (1 - e) + o * e
+        xx = o * (1 - e) + a * e
+        return (yy * side + xx) * 2 + e
+
+    def token_row(s, rel, d):
+        e = core if rel == 0 else 1 - core
+        base = pos_own if rel == 0 else pos_par
+        q = (base + n - s) % n if d == 0 else (base + s) % n
+        return pl.multiple_of(index_of(e, q) * tok + half * d, half)
+
+    return me, core, pos_own, token_row, index_of
+
+
 def kernel(side, x_in_hbm, gy_in_hbm, ug_hbm, uu_hbm, wg_hbm, wu_hbm, wd_hbm, xin_hbm, gamma_hbm, gr_hbm, o_hbm, wo_hbm,
-           ds_out, do_v, acc_g, acc_u, acc_d, acc_o,
-           yb, xb, ugt, uut, ug, uu, wg, wu, wd, xin, gamma, gr, ov, wo,
+           ds_out, do_v, acc_g, acc_u, acc_d, acc_o, yb, ov, wo,
+           xb, ugt, uut, ug, uu, wg, wu, wd, xin, gamma, gr,
            g_s, du_g, du_u, z_s, own_part, pp_send, pp_recv, rs_send, rs_recv, acc0,
            do_acc, o_pair,
            y_rs, y_rr, y_ps, y_pr, x_rs, x_rr, x_ps, x_pr,
@@ -37,29 +65,9 @@
     half = tok // 2
     ct = hid // TILES
 
-    me = lax.axis_index("tp")
-    core = me % 2
-    chip = me // 2
-    cy, cx = chip // side, chip % side
-    diag = (cx + cy) % side
-    pos_own = side * (cy * (1 - core) + cx * core) + diag
-    pos_par = side * (cx * (1 - core) + cy * core) + diag
-
-    def index_of(e, q):
-        a, b = q // side, q % side
-        o = (b - a + side) % side
-        yy = a * (1 - e) + o * e
-        xx = o * (1 - e) + a * e
-        return (yy * side + xx) * 2 + e
-
+    me, core, pos_own, token_row, index_of = places(side, tok)
     partner = me + 1 - 2 * core
     nxt = (index_of(core, (pos_own + 1) % n), index_of(core, (pos_own + n - 1) % n))
-
-    def token_row(s, rel, d):
-        e = core if rel == 0 else 1 - core
-        base = pos_own if rel == 0 else pos_par
-        q = (base + n - s) % n if d == 0 else (base + s) % n
-        return pl.multiple_of(index_of(e, q) * tok + half * d, half)
 
     def remote(src, dst, ssem, rsem, dev):
         return pltpu.make_async_remote_copy(src_ref=src, dst_ref=dst, send_sem=ssem, recv_sem=rsem,
@@ -197,23 +205,23 @@
             def _():
                 pp_copy(k - 2).wait_send()
 
-        def body(c, carry):
-            cols = pl.ds(pl.multiple_of(c * ct, ct), ct)
+        def body(c):
+            cols = pl.ds(c * ct, ct)
             r = (dot(du_g[k], wg[:, cols], NN) + dot(du_u[k], wu[:, cols], NN)).astype(BF16)
             for i in range(2):
                 own_part[ks, pl.ds(i * tok, tok), cols] = r[i * 2 * tok:i * 2 * tok + tok]
                 pp_send[ks, pl.ds(i * tok, tok), cols] = r[i * 2 * tok + tok:(i + 1) * 2 * tok]
-            return carry
-        lax.fori_loop(lo, hi, body, 0)
+        for c in range(lo, hi):
+            body(c)
         if hi == TILES:
             pp_copy(k).start()
 
     def task_3(k):
-        def body(c, carry):
-            cols = pl.ds(pl.multiple_of(c * ct, ct), ct)
+        def body(c):
+            cols = pl.ds(c * ct, ct)
             acc_d[:, cols] += dot(z_s[...], yb[k % 3, :, cols], TN)
-            return carry
-        lax.fori_loop(0, TILES, body, 0)
+        for c in range(TILES):
+            body(c)
 
     def task_4(k, lo, hi):
         if lo in (0, TILES // 2):
@@ -221,13 +229,13 @@
             pair_wait(xb, x_sems, 2 * k, X_PIECES, part)
             pair_wait(xb, x_sems, 2 * k + 1, X_PIECES, part)
 
-        def body(c, carry):
-            cols = pl.ds(pl.multiple_of(c * ct, ct), ct)
+        def body(c):
+            cols = pl.ds(c * ct, ct)
             xt = xb[k % 3, :, cols]
             acc_g[:, cols] += dot(du_g[k], xt, TN)
             acc_u[:, cols] += dot(du_u[k], xt, TN)
-            return carry
-        lax.fori_loop(lo, hi, body, 0)
+        for c in range(lo, hi):
+            body(c)
 
     def rs_copy(j, d, c, pieces):
         rows, cols = pl.ds(d * half, half), cols_of(c, pieces)
@@ -372,10 +380,13 @@
     def s_step(u, carry):
         m = u // 2 - 1
 
-        @pl.when(jnp.logical_and(u >= 2, u % 2 == 0))
+        @pl.when(jnp.logical_and(between(u, 2, n), u % 2 == 0))
         def _():
             each(SUBS, lambda d, c, p: pair_copy(yb, s_sems, 2 * m, d, c, p).wait_recv())
             each(SUBS, lambda d, c, p: pair_copy(yb, s_sems, 2 * m + 1, d, c, p).wait_recv())
+
+        @pl.when(jnp.logical_and(between(u, 2, n - 1), u % 2 == 0))
+        def _():
             o_begin(m)
         for c in range(SUBS):
             for d in range(2):
@@ -403,11 +414,11 @@
                 forward(xb, x_sems, u + 3, X_PIECES, (late[c // 2],))
 
             if c % (2 * SUBS // TILES) == 0:
-                @pl.when(u >= 2)
+                @pl.when(between(u, 2, n - 1))
                 def _():
                     o_task(m, (u % 2) * (TILES // 2) + c * TILES // (2 * SUBS))
 
-        @pl.when(jnp.logical_and(u >= 2, u % 2 == 1))
+        @pl.when(jnp.logical_and(between(u, 2, n - 1), u % 2 == 1))
         def _():
             o_end(m)
 
@@ -435,13 +446,14 @@
     ring = [dma((2, PIECES, SLOTS)) for _ in range(4)] + [dma((2, X_PIECES, SLOTS)) for _ in range(4)] + [dma((2, SUBS, 4)) for _ in range(4)]
     sems = ring + [dma((2, PIECES, 2)), dma((2, PIECES, 3)), dma((2,)), dma((2,)), dma((12,))]
     out_shape = (pltpu.VMEM((tok, hid), BF16), pltpu.VMEM((rows, ol), BF16), pltpu.VMEM((fl, hid), F32),
-                 pltpu.VMEM((fl, hid), F32), pltpu.VMEM((fl, hid), F32), pltpu.VMEM((ol, hid), F32))
+                 pltpu.VMEM((fl, hid), F32), pltpu.VMEM((fl, hid), F32), pltpu.VMEM((ol, hid), F32),
+                 pltpu.VMEM((3, 4 * tok, hid), BF16), pltpu.VMEM((rows, ol), BF16), pltpu.VMEM((ol, hid), BF16))
     v = pltpu.VMEM
     blk = 4 * tok
     scratch = [
-        v((3, blk, hid), BF16), v((3, blk, hid), BF16), v((fl, rows), BF16), v((fl, rows), BF16), v((rows, fl), BF16), v((rows, fl), BF16),
+        v((3, blk, hid), BF16), v((fl, rows), BF16), v((fl, rows), BF16), v((rows, fl), BF16), v((rows, fl), BF16),
         v((fl, hid), BF16), v((fl, hid), BF16), v((fl, hid), BF16), v((tok, hid), BF16), v((hid,), BF16),
-        v((tok, hid), BF16), v((rows, ol), BF16), v((ol, hid), BF16),
+        v((tok, hid), BF16),
         v((blk, fl), F32), v((rows // blk, blk, fl), BF16), v((rows // blk, blk, fl), BF16), v((blk, fl), BF16),
         v((2, 2 * tok, hid), BF16), v((2, 2 * tok, hid), BF16), v((2, 2 * tok, hid), BF16),
         v((2, tok, hid), BF16), v((3, tok, hid), BF16), v((tok, hid), F32),
@@ -451,29 +463,55 @@
         functools.partial(kernel, side),
         out_shape=out_shape,
         in_specs=[anyspec] * 12,
-        out_specs=tuple([pl.BlockSpec(memory_space=pltpu.VMEM)] * 6),
+        out_specs=tuple([pl.BlockSpec(memory_space=pltpu.VMEM)] * 9),
         scratch_shapes=scratch + sems,
-        compiler_params=pltpu.CompilerParams(collective_id=0, has_side_effects=True, vmem_limit_bytes=46800000),
+        compiler_params=pltpu.CompilerParams(collective_id=0, has_side_effects=True, vmem_limit_bytes=MEGA_VMEM),
     )(*args)
 
 
-def flush_kernel(*refs):
-    k = len(refs) // 2
-    copies = [pltpu.make_async_copy(refs[i], refs[k + i], refs[-1].at[i]) for i in range(k)]
+def flush_kernel(side, ds, do_v, acc_g, acc_u, acc_d, acc_o, yb, ov, wo,
+                 ds_hbm, do_hbm, dwg_hbm, dwu_hbm, dwd_hbm, dwo_hbm, do_last, o_pair, sums, sem, row_sem, col_sem):
+    n = side * side
+    tok, hid = ds.shape
+    half, ct, m = tok // 2, hid // TILES, n // 2 - 1
+    token_row = places(side, tok)[3]
+    pairs = ((do_v, do_hbm), (ds, ds_hbm), (acc_g, dwg_hbm), (acc_u, dwu_hbm), (acc_d, dwd_hbm))
+    copies = [pltpu.make_async_copy(a, b, sem.at[i]) for i, (a, b) in enumerate(pairs)]
     for c in copies:
         c.start()
-    for c in copies:
+    spots = [(i * 2 * tok + rel * tok + d * half, token_row(2 * m + i, rel, d))
+             for i in range(2) for rel in range(2) for d in range(2)]
+    for r0, row in spots:
+        o_pair[pl.ds(r0, half), :] = ov[pl.ds(row, half), :]
+    col_copies = []
+    for c in range(TILES):
+        cols = pl.ds(c * ct, ct)
+        sums[:, cols] = acc_o[:, cols] + dot(o_pair[...], yb[m % 3, :, cols], TN)
+        col_copies.append(pltpu.make_async_copy(sums.at[:, cols], dwo_hbm.at[:, cols], col_sem.at[c]))
+        col_copies[-1].start()
+    do_last[...] = dot(yb[m % 3], wo[...], NT).astype(BF16)
+    copies[0].wait()
+    row_copies = [pltpu.make_async_copy(do_last.at[pl.ds(r0, half), :], do_hbm.at[pl.ds(row, half), :], row_sem.at[i])
+                  for i, (r0, row) in enumerate(spots)]
+    for c in row_copies:
+        c.start()
+    for c in copies[1:] + col_copies + row_copies:
         c.wait()
 
 
-def flush(*arrays):
+def flush(side, *arrays):
+    outs = arrays[:6]
+    tok, hid = outs[0].shape
+    ol = outs[5].shape[0]
+    dma = pltpu.SemaphoreType.DMA
     return pl.pallas_call(
-        flush_kernel,
-        out_shape=tuple(pltpu.HBM(a.shape, a.dtype) for a in arrays),
+        functools.partial(flush_kernel, side),
+        out_shape=tuple(pltpu.HBM(a.shape, a.dtype) for a in outs),
         in_specs=[pl.BlockSpec(memory_space=pltpu.VMEM)] * len(arrays),
-        out_specs=tuple([pl.BlockSpec(memory_space=pltpu.HBM)] * len(arrays)),
-        scratch_shapes=[pltpu.SemaphoreType.DMA((len(arrays),))],
-        compiler_params=pltpu.CompilerParams(vmem_limit_bytes=1000000),
+        out_specs=tuple([pl.BlockSpec(memory_space=pltpu.HBM)] * len(outs)),
+        scratch_shapes=[pltpu.VMEM((4 * tok, ol), BF16), pltpu.VMEM((4 * tok, ol), BF16), pltpu.VMEM((ol, hid), F32),
+                        dma((5,)), dma((8,)), dma((TILES,))],
+        compiler_params=pltpu.CompilerParams(vmem_limit_bytes=FLUSH_VMEM),
     )(*[pltpu.with_memory_space_constraint(a, pltpu.VMEM) for a in arrays])
 
 
@@ -485,7 +523,7 @@
     side = math.isqrt(mesh.shape["tp"] // 2)
 
     def local_backward(x_norm, grad_y, u_gate, u_up, w_gate, w_up, w_down, x_in, gamma, grad_res, attn_out, w_out):
-        grad_sum, grad_attn, gw_gate, gw_up, gw_down, gw_out = flush(*mega(
+        grad_sum, grad_attn, gw_gate, gw_up, gw_down, gw_out = flush(side, *mega(
             side, x_norm, grad_y, u_gate.T, u_up.T, w_gate.T, w_up.T, w_down, x_in, gamma,
             grad_res, attn_out, w_out))
         return grad_sum, grad_attn, gw_gate.T, gw_up.T, gw_down, gw_out

time: 210 us -> 206 us (0.981)
  Pallas kernels: 209 us -> 205 us
    pallas_call x1, Pallas kernels: 202 us -> 198 us  [mega(): pl.pallas_call(functools.partial(kernel, side), out_shape=out_shape, in_s...]
where the time goes in v5:
time: 206 us
  Pallas kernels  205 us (100%)
    pallas_call x1, Pallas kernels, mega(): pl.pallas_call(functools.partial(kernel, side), out_shape=out_shape, in_s...  198 us
    pallas_call x1, Pallas kernels, flush(): pl.pallas_call(functools.partial(flush_kernel, side), out_shape=tuple((pl...  7.64 us

profile of v5, /device:TPU:97, one launch (start us, length us, event | category | flops | bytes accessed | tf_op | source)
XLA Modules:
  0.0 206.1 jit_solution(12016541518510555272)
XLA Ops:
  0.6 197.6 %shard_map.163 = (bf16[64,4096]{1,0:T(8,128)(2,1)S(1)}, bf16[2048,128]{1,0:T(8,128)(2,1)S(1)}, f32[344,4096]{1,0:T(8,128)S(1)}, f32[344,4096]{1,0:T(8,128)S(1)},...) custom-call(bf16[64,4096]{1,0:T(8,128)(2,1)} %x_in_hbm.1, ...), custom_call_target="tpu_custom_call" | custom-call | tf_op jit(solution)/shard_map/pallas_call | solution.py:462
  198.3 7.6 %shard_map.164 = (bf16[64,4096]{1,0:T(8,128)(2,1)}, bf16[2048,128]{1,0:T(8,128)(2,1)}, f32[344,4096]{1,0:T(8,128)}, f32[344,4096]{1,0:T(8,128)}, f32[344,4096]{1,0:T(8,128)}, /*index=5*/f32[128,4096]{1,0:T(8,128)}) custom-call(bf16[64,4096]{1,0:T(8,128)(2,1)S(1)} %get-tuple-element.21.ds, bf16[2048,128]{1,0:T(8,128)(2,1)S(1)} %get-tuple-element.22.do_v, ...), custom_call_target="tpu_custom_call" | custom-call | tf_op jit(solution)/shard_map/pallas_call | solution.py:507
